TPU v7x, 32 devices: a whole 2x2x4 slice. The times are simulated.
32 devices in a mesh: dp: 8 (over y, x, core), mp: 4 (over z).
Axes of the slice: x: 2, y: 2, z: 4, core: 2. Of those that a mesh axis runs over, the one named last changes fastest.
Arguments:
- tokens: bfloat16 [8192, 2048], P('dp'), may hold values from -6 to 6
- cotangent: bfloat16 [8192, 2048], P('dp'), may hold values from -6 to 6
- counts: int32 [8], replicated, may hold values from 1 to 1024, 5120 in all
- w_qkv: bfloat16 [2048, 3, 2048], P('dp', None, 'mp'), may hold values from -0.125 to 0.125
- w_out: bfloat16 [2048, 2048], P('mp', 'dp'), may hold values from -1 to 1
- w_fc1: bfloat16 [2048, 8192], P('dp', 'mp'), may hold values from -0.125 to 0.125
- w_fc2: bfloat16 [8192, 2048], P('mp', 'dp'), may hold values from -0.0625 to 0.0625
- ln1_gain: bfloat16 [2048], P('dp'), may hold values from 0.5 to 1.5
- ln1_bias: bfloat16 [2048], P('dp'), may hold values from -1.796875 to 1.796875
- ln2_gain: bfloat16 [2048], P('dp'), may hold values from 0.5 to 1.5
- ln2_bias: bfloat16 [2048], P('dp'), may hold values from -1.796875 to 1.796875
- qv_bias: bfloat16 [2, 2048], P(None, ('mp', 'dp')), may hold values from -1.796875 to 1.796875
- out_bias: bfloat16 [2048], P('dp'), may hold values from -1.796875 to 1.796875
- fc1_bias: bfloat16 [8192], P(('mp', 'dp')), may hold values from -1.796875 to 1.796875
- fc2_bias: bfloat16 [2048], P('dp'), may hold values from -1.796875 to 1.796875
Outputs:
- out_tokens: bfloat16 [8192, 2048], P('dp')
- grad_tokens: float32 [8192, 2048], P('dp')
- grad_w_qkv: float32 [2048, 3, 2048], P('dp', None, 'mp')
- grad_w_out: float32 [2048, 2048], P('mp', 'dp')
- grad_w_fc1: float32 [2048, 8192], P('dp', 'mp')
- grad_w_fc2: float32 [8192, 2048], P('mp', 'dp')
- grad_ln1_gain: float32 [2048], P('dp')
- grad_ln1_bias: float32 [2048], P('dp')
- grad_ln2_gain: float32 [2048], P('dp')
- grad_ln2_bias: float32 [2048], P('dp')
- grad_qv_bias: float32 [2, 2048], P(None, ('mp', 'dp'))
- grad_out_bias: float32 [2048], P('dp')
- grad_fc1_bias: float32 [8192], P(('mp', 'dp'))
- grad_fc2_bias: float32 [2048], P('dp')
Inputs may be any that keep to these rules, and one draw needn't show every extreme that they name: counts[g] is the number of live tokens of group g's sequence, at the start of its 1024 slots; the largest count equals 1024.
All inputs are finite; a program needn't handle non-finite values.
Results may differ from a plain program's by a relative error of at most 0.014.
Values may be sent and summed in bfloat16 or wider, within the bound.
A program may use at most 192 MiB of HBM per device.

v0:
```python
import math

import jax
import jax.numpy as jnp
from jax import lax
from jax.sharding import PartitionSpec as P

HEAD = 128


EPS = 1e-05
NEG = -1e30


def layer_norm(values, gain_vec, shift_vec):
    center = values - jnp.mean(values, axis=-1, keepdims=True)
    spread = jnp.mean(center * center, axis=-1, keepdims=True)
    return center * lax.rsqrt(spread + EPS) * gain_vec + shift_vec


def smooth_gate(values):
    return jax.nn.gelu(values, approximate=True)


def causal_scores(queries, key_heads, inv_root):
    row_count = queries.shape[0]
    raw_scores = (
        jnp.einsum("qhd,khd->hqk", queries, key_heads, preferred_element_type=jnp.float32)
        * inv_root
    )
    future = lax.broadcasted_iota(jnp.int32, (row_count, row_count), 1) > lax.broadcasted_iota(
        jnp.int32, (row_count, row_count), 0
    )
    return jnp.where(future[None], NEG, raw_scores)


def shards(
    tokens,
    cotangent,
    counts,
    w_qkv,
    w_out,
    w_fc1,
    w_fc2,
    ln1_gain,
    ln1_bias,
    ln2_gain,
    ln2_bias,
    qv_bias,
    out_bias,
    fc1_bias,
    fc2_bias,
):
    gathered = (
        lax.all_gather(w_qkv, "dp", axis=0, tiled=True),
        lax.all_gather(w_out, "dp", axis=1, tiled=True),
        lax.all_gather(w_fc1, "dp", axis=0, tiled=True),
        lax.all_gather(w_fc2, "dp", axis=1, tiled=True),
        lax.all_gather(ln1_gain, "dp", axis=0, tiled=True),
        lax.all_gather(ln1_bias, "dp", axis=0, tiled=True),
        lax.all_gather(ln2_gain, "dp", axis=0, tiled=True),
        lax.all_gather(ln2_bias, "dp", axis=0, tiled=True),
        lax.all_gather(qv_bias, "dp", axis=1, tiled=True),
        lax.all_gather(out_bias, "dp", axis=0, tiled=True),
        lax.all_gather(fc1_bias, "dp", axis=0, tiled=True),
        lax.all_gather(fc2_bias, "dp", axis=0, tiled=True),
    )
    whole_qkv, whole_out, whole_fc1, whole_fc2 = (
        gathered[0],
        gathered[1],
        gathered[2],
        gathered[3],
    )
    gain_one = gathered[4].astype(jnp.float32)
    shift_one = gathered[5].astype(jnp.float32)
    gain_two = gathered[6].astype(jnp.float32)
    shift_two = gathered[7].astype(jnp.float32)
    bias_qv = gathered[8].astype(jnp.float32)
    bias_out = gathered[9].astype(jnp.float32)
    bias_fc1 = gathered[10].astype(jnp.float32)
    bias_fc2 = gathered[11].astype(jnp.float32)
    seq_rows = tokens.shape[0]
    local_width = whole_qkv.shape[2]
    heads_here = local_width // HEAD
    inv_root = 1.0 / math.sqrt(HEAD)
    inputs = tokens.astype(jnp.float32)
    normed_one = layer_norm(inputs, gain_one, shift_one).astype(jnp.bfloat16)
    projected = jnp.einsum("sd,dce->sce", normed_one, whole_qkv, preferred_element_type=jnp.float32)
    queries = (
        (projected[:, 0] + bias_qv[0]).astype(jnp.bfloat16).reshape(seq_rows, heads_here, HEAD)
    )
    key_heads = projected[:, 1].astype(jnp.bfloat16).reshape(seq_rows, heads_here, HEAD)
    values = (projected[:, 2] + bias_qv[1]).astype(jnp.bfloat16).reshape(seq_rows, heads_here, HEAD)
    scores = causal_scores(queries, key_heads, inv_root)
    row_peak = jnp.max(scores, axis=-1, keepdims=True)
    exp_terms = jnp.exp(scores - row_peak)
    exp_total = jnp.sum(exp_terms, axis=-1, keepdims=True)
    log_total = row_peak + jnp.log(exp_total)
    prob_low = (exp_terms / exp_total).astype(jnp.bfloat16)
    mixed_heads = (
        jnp.einsum("hqk,khd->qhd", prob_low, values, preferred_element_type=jnp.float32)
        .astype(jnp.bfloat16)
        .reshape(seq_rows, local_width)
    )
    attn_part = jnp.dot(mixed_heads, whole_out, preferred_element_type=jnp.float32)
    residual = inputs + lax.psum(attn_part, "mp") + bias_out
    normed_two = layer_norm(residual, gain_two, shift_two).astype(jnp.bfloat16)
    preact = jnp.dot(normed_two, whole_fc1, preferred_element_type=jnp.float32) + bias_fc1
    activated = smooth_gate(preact).astype(jnp.bfloat16)
    ffn_part = jnp.dot(activated, whole_fc2, preferred_element_type=jnp.float32)
    out_tokens = (
        residual + lax.psum(ffn_part.astype(jnp.bfloat16), "mp").astype(jnp.float32) + bias_fc2
    ).astype(jnp.bfloat16)
    dp_index = lax.axis_index("dp")
    slot_ids = lax.iota(jnp.int32, counts.shape[0])
    own_count = jnp.sum(jnp.where(slot_ids == dp_index, counts, 0))
    weight_share = own_count.astype(jnp.float32) / jnp.sum(counts).astype(jnp.float32)
    live_rows = lax.iota(jnp.int32, seq_rows) < own_count
    grad_out = jnp.where(live_rows[:, None], cotangent.astype(jnp.float32), 0.0)
    grad_out_low = grad_out.astype(jnp.bfloat16)
    grad_fc2 = (
        jnp.einsum("sf,sd->fd", activated, grad_out_low, preferred_element_type=jnp.float32)
        * weight_share
    )
    grad_fc2_bias = jnp.sum(grad_out, axis=0) * weight_share
    delta_act = jnp.einsum("sd,fd->sf", grad_out_low, whole_fc2, preferred_element_type=jnp.float32)
    unused_gate, gate_back = jax.vjp(smooth_gate, preact)
    delta_pre = gate_back(delta_act)[0]
    grad_fc1_bias = jnp.sum(delta_pre, axis=0) * weight_share
    delta_pre_low = delta_pre.astype(jnp.bfloat16)
    grad_fc1 = (
        jnp.einsum("sd,sf->df", normed_two, delta_pre_low, preferred_element_type=jnp.float32)
        * weight_share
    )
    two_part = jnp.einsum("sf,df->sd", delta_pre_low, whole_fc1, preferred_element_type=jnp.float32)
    delta_two = lax.psum(two_part, "mp")
    unused_two, second_back = jax.vjp(layer_norm, residual, gain_two, shift_two)
    resid_part, gain_two_part, shift_two_part = second_back(delta_two)
    delta_resid = resid_part + grad_out
    delta_resid_low = delta_resid.astype(jnp.bfloat16)
    out_bias_part = jnp.sum(delta_resid, axis=0)
    grad_out_proj = (
        jnp.einsum("sc,sd->cd", mixed_heads, delta_resid_low, preferred_element_type=jnp.float32)
        * weight_share
    )
    delta_mixed = jnp.einsum(
        "sd,cd->sc", delta_resid_low, whole_out, preferred_element_type=jnp.float32
    )
    delta_mixed_low = delta_mixed.astype(jnp.bfloat16).reshape(seq_rows, heads_here, HEAD)
    scores_again = causal_scores(queries, key_heads, inv_root)
    prob_full = jnp.exp(scores_again - log_total)
    delta_prob = jnp.einsum(
        "qhd,khd->hqk", delta_mixed_low, values, preferred_element_type=jnp.float32
    )
    delta_scores = prob_full * (
        delta_prob - jnp.sum(prob_full * delta_prob, axis=-1, keepdims=True)
    )
    delta_scores_low = delta_scores.astype(jnp.bfloat16)
    delta_q = (
        jnp.einsum("hqk,khd->qhd", delta_scores_low, key_heads, preferred_element_type=jnp.float32)
        * inv_root
    ).reshape(seq_rows, local_width)
    delta_k = (
        jnp.einsum("hqk,qhd->khd", delta_scores_low, queries, preferred_element_type=jnp.float32)
        * inv_root
    ).reshape(seq_rows, local_width)
    delta_v = jnp.einsum(
        "hqk,qhd->khd", prob_low, delta_mixed_low, preferred_element_type=jnp.float32
    ).reshape(seq_rows, local_width)
    grad_qv = jnp.stack([jnp.sum(delta_q, axis=0), jnp.sum(delta_v, axis=0)]) * weight_share
    delta_proj = jnp.stack([delta_q, delta_k, delta_v], axis=1).astype(jnp.bfloat16)
    grad_qkv = (
        jnp.einsum("sd,sce->dce", normed_one, delta_proj, preferred_element_type=jnp.float32)
        * weight_share
    )
    one_part = jnp.einsum("sce,dce->sd", delta_proj, whole_qkv, preferred_element_type=jnp.float32)
    delta_one = lax.psum(one_part.astype(jnp.bfloat16), "mp").astype(jnp.float32)
    unused_one, first_back = jax.vjp(layer_norm, inputs, gain_one, shift_one)
    input_part, gain_one_part, shift_one_part = first_back(delta_one)
    grad_tokens = input_part + delta_resid
    stat_sums = jnp.stack(
        [gain_two_part, shift_two_part, out_bias_part, gain_one_part, shift_one_part]
    )
    stat_weighted = stat_sums * weight_share
    summed_all = (
        lax.psum_scatter(grad_qkv, "dp", scatter_dimension=0, tiled=True),
        lax.psum_scatter(grad_out_proj, "dp", scatter_dimension=1, tiled=True),
        lax.psum_scatter(grad_qv, "dp", scatter_dimension=1, tiled=True),
        lax.psum_scatter(stat_weighted[2], "dp", scatter_dimension=0, tiled=True),
        lax.psum_scatter(stat_weighted[3], "dp", scatter_dimension=0, tiled=True),
        lax.psum_scatter(stat_weighted[4], "dp", scatter_dimension=0, tiled=True),
        lax.psum_scatter(grad_fc1, "dp", scatter_dimension=0, tiled=True),
        lax.psum_scatter(grad_fc2, "dp", scatter_dimension=1, tiled=True),
        lax.psum_scatter(grad_fc1_bias, "dp", scatter_dimension=0, tiled=True),
        lax.psum_scatter(grad_fc2_bias, "dp", scatter_dimension=0, tiled=True),
        lax.psum_scatter(stat_weighted[0], "dp", scatter_dimension=0, tiled=True),
        lax.psum_scatter(stat_weighted[1], "dp", scatter_dimension=0, tiled=True),
    )
    return (
        out_tokens,
        grad_tokens,
        summed_all[0],
        summed_all[1],
        summed_all[6],
        summed_all[7],
        summed_all[4],
        summed_all[5],
        summed_all[10],
        summed_all[11],
        summed_all[2],
        summed_all[3],
        summed_all[8],
        summed_all[9],
    )


def solution(mesh):
    placed = (
        P("dp", None),
        P("dp", None),
        P(),
        P("dp", None, "mp"),
        P("mp", "dp"),
        P("dp", "mp"),
        P("mp", "dp"),
        P("dp"),
        P("dp"),
        P("dp"),
        P("dp"),
        P(None, ("mp", "dp")),
        P("dp"),
        P(("mp", "dp")),
        P("dp"),
    )
    return jax.shard_map(
        shards,
        mesh=mesh,
        in_specs=placed,
        out_specs=(
            P("dp", None),
            P("dp", None),
            P("dp", None, "mp"),
            P("mp", "dp"),
            P("dp", "mp"),
            P("mp", "dp"),
            P("dp"),
            P("dp"),
            P("dp"),
            P("dp"),
            P(None, ("mp", "dp")),
            P("dp"),
            P(("mp", "dp")),
            P("dp"),
        ),
        check_vma=False,
    )
```

profile of v0, /device:TPU:0, one launch (start us, length us, event | category | flops | bytes accessed | tf_op | source)
XLA Modules:
  0.0 1626.7 jit_solution(16595095688366546610)
XLA Ops:
  12.0 10.4 all-gather.2
  25.3 3.4 fusion.15
  28.8 8.9 all-gather.1
  37.7 8.9 all-gather
  46.6 13.2 all-gather.13.cloned.1.call-done
  59.8 10.4 fusion.38
  72.1 7.7 fusion.57
  79.8 8.1 fusion
  89.9 8.1 divide_convert_fusion
  98.1 3.2 copy-done.2
  102.8 7.7 fusion.59
  111.8 9.1 all-gather.6
  120.9 8.0 all-gather.3
  129.0 8.9 all-gather.5
  137.9 8.0 all-gather.4
  147.2 254.6 %all-reduce.13.cloned.1.call-done = f32[1024,2048]{1,0:T(8,128)} async-done(((f32[1024,2048]{1,0:T(8,128)}), f32[1024,2048]{1,0:T(8,128)}) %all-reduce.13.cloned.1.call-update) | async-done | bytes 8388624 | tf_op jit(solution)/shard_map/psum | solution.py:106
  401.8 5.7 fusion.52
  407.5 3.5 copy-done
  412.0 44.7 %all-gather.17.cloned.1.call-done = bf16[2048,2048]{1,0:T(8,128)(2,1)} async-done(((bf16[256,2048]{1,0:T(8,128)(2,1)}), bf16[2048,2048]{1,0:T(8,128)(2,1)}) %all-gather.17.cloned.1.call-update) | async-done | bytes 8388624 | tf_op jit(solution)/shard_map/all_gather | solution.py:57
  456.8 16.0 fusion.48
  472.8 41.6 %all-gather.19.cloned.1.call-done = bf16[2048,2048]{1,0:T(8,128)(2,1)} async-done(((bf16[2048,256]{1,0:T(8,128)(2,1)}), bf16[2048,2048]{1,0:T(8,128)(2,1)}) %all-gather.19.cloned.1.call-update) | async-done | bytes 8388624 | tf_op jit(solution)/shard_map/all_gather | solution.py:58
  514.4 20.5 %fusion.58 = (f32[2048]{0:T(1024)}, bf16[1024,2048]{1,0:T(8,128)(2,1)S(1)}) fusion(f32[1024,2048]{1,0:T(8,128)} %fusion.48, f32[2048]{0:T(1024)S(1)} %bitcast.123, bf16[2048,2048]{1,0:T(8,128)(2,1)} %all-gather.19.cloned.1.call-done, bf16[1024,2048]{1,0:T(8,128)(2,1)} %param.16, pred[1024]{0:T(1024)(128)(4,1)S(1)} %iota_compare_fusion.1), kind=kOutput, calls=%fused_computation.107 | convolution fusion | flops 8642361344 | bytes 25183232 | tf_op jit(solution)/shard_map/sd,fd->sf/dot_general | solution.py:126
  536.9 13.2 fusion.27
  551.5 17.2 %convolution_convert_fusion = bf16[1024,2048]{1,0:T(8,128)(2,1)} fusion(bf16[2048,2048]{1,0:T(8,128)(2,1)} %all-gather.19.cloned.1.call-done, f32[1024,2048]{1,0:T(8,128)} %fusion.48, f32[2048]{0:T(1024)S(1)} %bitcast.124), kind=kOutput, calls=%fused_computation.53 | convolution fusion | flops 8613003264 | bytes 20979712 | tf_op jit(solution)/shard_map/dot_general | solution.py:110
  568.7 272.4 %all-reduce.15.cloned.1.call-done = f32[1024,2048]{1,0:T(8,128)} async-done(((f32[1024,2048]{1,0:T(8,128)}), f32[1024,2048]{1,0:T(8,128)}) %all-reduce.15.cloned.1.call-update) | async-done | bytes 8388624 | tf_op jit(solution)/shard_map/psum | solution.py:136
  841.1 8.0 multiply_reduce_fusion.1
  849.3 4.9 fusion.51
  854.3 6.7 fusion.34
  861.0 2.9 bitcast_convert_fusion.1
  864.0 10.6 multiply_reduce_fusion
  874.6 12.2 multiply_convert_fusion
  886.9 3.9 multiply_convert_fusion.2
  890.7 3.0 bitcast_convert_fusion.2
  901.6 11.0 bitcast_convert_fusion
  913.8 9.2 convolution_multiply_fusion.2
  923.1 17.6 %convolution_multiply_fusion = f32[2048,2048]{1,0:T(8,128)} fusion(f32[]{:T(128)S(6)} %div.63, bf16[1024,2048]{1,0:T(8,128)(2,1)} %param.16, pred[1024]{0:T(1024)(128)(4,1)S(1)} %iota_compare_fusion.1, f32[1024,2048]{1,0:T(8,128)} %fusion.48, f32[2048]{0:T(1024)S(1)} %bitcast.125), kind=kOutput, calls=%fused_computation.23 | convolution fusion | flops 8621391872 | bytes 29369348 | tf_op jit(solution)/shard_map/sf,sd->fd/dot_general | solution.py:122
  941.4 17.1 %convolution_multiply_fusion.1 = f32[2048,2048]{1,0:T(8,128)} fusion(f32[]{:T(128)S(6)} %div.63, bf16[1024,2048]{1,0:T(8,128)(2,1)} %copy-done.43, f32[1024,2048]{1,0:T(8,128)} %copy-done, f32[2048]{0:T(1024)S(1)} %bitcast.122, f32[2048]{0:T(1024)S(1)} %bitcast.98, f32[1024]{0:T(1024)S(1)} %fusion.42, f32[1024]{0:T(1024)S(1)} %broadcast_multiply_fusion.4), kind=kOutput, calls=%fused_computation.24 | convolution fusion | flops 8604614656 | bytes 29384708 | tf_op jit(solution)/shard_map/sd,sf->df/dot_general | solution.py:132
  959.8 13.7 broadcast_multiply_fusion
  974.2 8.9 all-gather.7
  985.8 242.6 %all-reduce.17.cloned.1.call-done = (bf16[1024,2048]{1,0:T(8,128)(2,1)}, bf16[1024,2048]{1,0:T(8,128)(2,1)}) async-done(((bf16[1024,2048]{1,0:T(8,128)(2,1)}, bf16[1024,2048]{1,0:T(8,128)(2,1)}), (bf16[1024,2048]{1,0:T(8,128)(2,1)}, bf16[1024,2048]{1,0:T(8,128)(2,1)})) %all-reduce.17.cloned.1.call-update) | async-done | bytes 8388624 | tf_op jit(solution)/shard_map/psum | solution.py:112
  1228.4 5.6 convert_reduce_fusion
  1234.3 4.4 fusion.18
  1238.8 10.4 fusion.19
  1249.3 25.4 %all-reduce.7 = (f32[2048]{0:T(1024)S(1)}, f32[2048]{0:T(1024)S(1)}, f32[2048]{0:T(1024)S(1)}, f32[2048]{0:T(1024)S(1)}, f32[2048]{0:T(1024)S(1)}, /*index=5*/f32[2048]{0:T(1024)S(1)}, f32[2048]{0:T(1024)S(1)}) all-reduce(f32[2048]{0:T(1024)S(1)} %bitcast.111, f32[2048]{0:T(1024)S(1)} %bitcast.110, ...), channel_id=6, replica_groups=mesh['dp'=8,'mp'=4] {'dp'}, use_global_device_ids=true, to_apply=%region_26.27.clone | all-reduce | flops 14336 | bytes 114688
  1279.2 8.5 add_convert_fusion
  1287.7 115.5 %reduce-scatter.14.cloned.1.call-done = f32[2048,256]{1,0:T(8,128)} async-done(((f32[2048,2048]{1,0:T(8,128)}), f32[2048,256]{1,0:T(8,128)}) %reduce-scatter.14.cloned.1.call-update) | async-done | bytes 2097168 | tf_op jit(solution)/shard_map/reduce_scatter | solution.py:193
  1403.2 120.4 %reduce-scatter.12.cloned.1.call-done = f32[256,2048]{1,0:T(8,128)} async-done(((f32[2048,2048]{1,0:T(8,128)}), f32[256,2048]{1,0:T(8,128)}) %reduce-scatter.12.cloned.1.call-update) | async-done | bytes 2097168 | tf_op jit(solution)/shard_map/reduce_scatter | solution.py:192
  1523.5 96.0 %reduce-scatter.8.cloned.1.call-done = f32[256,3,512]{2,0,1:T(8,128)} async-done(((f32[2048,3,512]{2,0,1:T(8,128)}), f32[256,3,512]{2,0,1:T(8,128)}) %reduce-scatter.8.cloned.1.call-update) | async-done | bytes 1572880 | tf_op jit(solution)/shard_map/reduce_scatter | solution.py:186
  (175 shorter events, 37.3 us)
Async XLA Ops:
  7.2 52.6 %all-gather.13.cloned.1.call-start = ((), (), s32[]{:S(2)}) async-start(), calls=%async_computation.5 | async-start | bytes 7077888 | tf_op jit(solution)/shard_map/all_gather | solution.py:55
  9.5 93.2 %all-gather.15.cloned.1.call-start = ((), (), s32[]{:S(2)}) async-start(), calls=%async_computation.6 | async-start | bytes 2359296 | tf_op jit(solution)/shard_map/all_gather | solution.py:56
  10.3 391.5 %all-reduce.13.cloned.1.call-start = ((), (), s32[]{:S(2)}) async-start(), calls=%async_computation.7 | async-start | bytes 16777216 | tf_op jit(solution)/shard_map/psum | solution.py:106
  22.4 49.7 %copy-start.29 = (f32[1,512]{1,0:T(1,128)}, f32[1,512]{1,0:T(1,128)S(1)}, u32[]{:S(2)}) copy-start(f32[1,512]{1,0:T(1,128)S(1)} %get-tuple-element.47) | copy-start | bytes 6148
  25.3 44.9 %copy-start.21 = (f32[1024]{0:T(1024)}, f32[1024]{0:T(1024)S(1)}, u32[]{:S(2)}) copy-start(f32[1024]{0:T(1024)S(1)} %broadcast_multiply_fusion.5) | copy-start | bytes 12292
  28.8 8.9 copy-start.25
  28.8 41.5 %copy-start.23 = (f32[1024]{0:T(1024)}, f32[1024]{0:T(1024)S(1)}, u32[]{:S(2)}) copy-start(f32[1024]{0:T(1024)S(1)} %fusion.41) | copy-start | bytes 12292
  37.7 32.6 %copy-start.31 = (f32[8,1,256]{2,1,0:T(1,128)}, f32[8,1,256]{2,1,0:T(1,128)S(1)}, u32[]{:S(2)}) copy-start(f32[8,1,256]{2,1,0:T(1,128)S(1)} %convert_element_type.130) | copy-start | bytes 24580
  46.5 23.7 %copy-start.19 = (f32[8,1,256]{2,1,0:T(1,128)}, f32[8,1,256]{2,1,0:T(1,128)S(1)}, u32[]{:S(2)}) copy-start(f32[8,1,256]{2,1,0:T(1,128)S(1)} %convert_element_type.129) | copy-start | bytes 24580
  70.4 9.3 copy-start.10
  72.1 7.7 copy-start.6
  89.9 8.1 copy-start.8
  98.0 3.2 copy-start.2
  102.7 7.8 copy-start.14
  110.5 1.3 copy-start.39
  110.5 1.3 copy-start.40
  110.5 35.4 %copy-start.36 = (s32[8]{0:T(128)S(1)}, s32[8]{0:T(128)}, u32[]{:S(2)}) copy-start(s32[8]{0:T(128)} %param.17) | copy-start | bytes 100
  110.5 346.2 %all-gather.17.cloned.1.call-start = ((), (), s32[]{:S(2)}) async-start(), calls=%async_computation.8 | async-start | bytes 9437184 | tf_op jit(solution)/shard_map/all_gather | solution.py:57
  111.1 403.3 %all-gather.19.cloned.1.call-start = ((), (), s32[]{:S(2)}) async-start(), calls=%async_computation.9 | async-start | bytes 9437184 | tf_op jit(solution)/shard_map/all_gather | solution.py:58
  111.7 729.4 %all-reduce.15.cloned.1.call-start = ((), (), s32[]{:S(2)}) async-start(), calls=%async_computation.10 | async-start | bytes 16777216 | tf_op jit(solution)/shard_map/psum | solution.py:136
  137.8 318.9 %copy-start.34 = (f32[8,1,256]{2,1,0:T(1,128)}, f32[8,1,256]{2,1,0:T(1,128)S(1)}, u32[]{:S(2)}) copy-start(f32[8,1,256]{2,1,0:T(1,128)S(1)} %convert_element_type.134) | copy-start | bytes 24580
  407.5 3.6 copy-start
  534.9 1.9 copy-start.43
  550.1 434.3 %reduce-scatter.16.cloned.1.call-start = ((), (), s32[]{:S(2)}) async-start(), calls=%async_computation.15 | async-start | bytes 294912
  841.1 8.2 copy-start.5
  849.3 5.0 copy-start.12
  849.3 11.7 slice-start
  854.3 6.7 copy-start.4
  854.3 6.7 slice-start.1
  861.0 3.0 copy-start.9
  874.6 12.2 copy-start.7
  874.6 12.3 copy-start.30
  886.8 3.9 copy-start.11
  895.1 6.5 copy-start.16
  898.4 3.2 copy-start.17
  901.5 326.9 %all-reduce.17.cloned.1.call-start = ((), (), s32[]{:S(2)}) async-start(), calls=%async_computation.16 | async-start | bytes 16777216 | tf_op jit(solution)/shard_map/psum | solution.py:112
  912.6 375.1 %reduce-scatter.10.cloned.1.call-start = ((), (), s32[]{:S(2)}) async-start(), calls=%async_computation.12 | async-start | bytes 4718592 | tf_op jit(solution)/shard_map/reduce_scatter | solution.py:187
  923.0 480.2 %reduce-scatter.14.cloned.1.call-start = ((), (), s32[]{:S(2)}) async-start(), calls=%async_computation.14 | async-start | bytes 18874368 | tf_op jit(solution)/shard_map/reduce_scatter | solution.py:193
  940.7 582.8 %reduce-scatter.12.cloned.1.call-start = ((), (), s32[]{:S(2)}) async-start(), calls=%async_computation.13 | async-start | bytes 18874368 | tf_op jit(solution)/shard_map/reduce_scatter | solution.py:192
  958.6 661.0 %reduce-scatter.8.cloned.1.call-start = ((), (), s32[]{:S(2)}) async-start(), calls=%async_computation.11 | async-start | bytes 14155776 | tf_op jit(solution)/shard_map/reduce_scatter | solution.py:186
  973.5 9.6 copy-start.42
  973.5 10.8 copy-start.33
  973.6 260.4 %copy-start.26 = (f32[1024]{0:T(1024)S(1)}, f32[1024]{0:T(1024)}, u32[]{:S(2)}) copy-start(f32[1024]{0:T(1024)} %copy-done.25) | copy-start | bytes 12292
  1228.4 5.6 copy-start.1
  1228.4 5.9 copy-start.3
  1228.4 10.4 copy-start.13
  1238.8 10.4 copy-start.27
  1238.8 10.4 copy-start.28
  (10 other events, 11.4 us)
Sparse Core Ops, SparseCore 0:
  10.4 49.3 all-gather.12
  61.7 28.0 all-gather.14
  110.7 291.0 all-reduce.12
  403.5 53.2 all-gather.16
  458.5 55.8 all-gather.18
  550.2 290.8 all-reduce.14
  901.6 32.6 reduce-scatter.15
  937.5 290.8 all-reduce.16
  1232.3 50.8 reduce-scatter.9
  1287.2 115.9 reduce-scatter.13
  1407.3 116.1 reduce-scatter.11
  1527.5 92.0 reduce-scatter.7
where the time goes:
time: 1630 us
  waiting for transfers between devices  1200 us (74%)
  matrix products  190 us (12%)
  blocking collectives  96.4 us (6%)
  other arithmetic  87.4 us (5%)
  local copies, waits for them, and re-layouts  32.2 us (2%)
  between operations  17.2 us (1%)
    psum x1, waiting for transfers between devices, shards(): delta_two = lax.psum(two_part, 'mp')  272 us
    psum x1, waiting for transfers between devices, shards(): residual = inputs + lax.psum(attn_part, 'mp') + bias_out  255 us
    psum x1, waiting for transfers between devices, shards(): lax.psum(ffn_part.astype(jnp.bfloat16), 'mp').astype(jnp.float32)  243 us
    reduce_scatter x1, waiting for transfers between devices, shards(): lax.psum_scatter(grad_fc1, 'dp', scatter_dimension=0, tiled=True)  120 us
    reduce_scatter x1, waiting for transfers between devices, shards(): lax.psum_scatter(grad_fc2, 'dp', scatter_dimension=1, tiled=True)  115 us
    reduce_scatter x1, waiting for transfers between devices, shards(): lax.psum_scatter(grad_qkv, 'dp', scatter_dimension=0, tiled=True)  96 us
    all_gather x1, waiting for transfers between devices, shards(): lax.all_gather(w_fc1, 'dp', axis=0, tiled=True)  44.7 us
    all_gather x1, waiting for transfers between devices, shards(): lax.all_gather(w_fc2, 'dp', axis=1, tiled=True)  41.6 us
  transfers between devices with their start and end apart: 12, of which 9 were waited for; matrix products, arithmetic and copies ran while one was open for 12% of the time, Pallas kernels for 0%

commit v1 on v0

--- a/solution.py
+++ b/solution.py
@@ -51,34 +51,31 @@
     fc1_bias,
     fc2_bias,
 ):
-    gathered = (
-        lax.all_gather(w_qkv, "dp", axis=0, tiled=True),
-        lax.all_gather(w_out, "dp", axis=1, tiled=True),
-        lax.all_gather(w_fc1, "dp", axis=0, tiled=True),
-        lax.all_gather(w_fc2, "dp", axis=1, tiled=True),
-        lax.all_gather(ln1_gain, "dp", axis=0, tiled=True),
-        lax.all_gather(ln1_bias, "dp", axis=0, tiled=True),
-        lax.all_gather(ln2_gain, "dp", axis=0, tiled=True),
-        lax.all_gather(ln2_bias, "dp", axis=0, tiled=True),
-        lax.all_gather(qv_bias, "dp", axis=1, tiled=True),
-        lax.all_gather(out_bias, "dp", axis=0, tiled=True),
-        lax.all_gather(fc1_bias, "dp", axis=0, tiled=True),
-        lax.all_gather(fc2_bias, "dp", axis=0, tiled=True),
-    )
-    whole_qkv, whole_out, whole_fc1, whole_fc2 = (
-        gathered[0],
-        gathered[1],
-        gathered[2],
-        gathered[3],
-    )
-    gain_one = gathered[4].astype(jnp.float32)
-    shift_one = gathered[5].astype(jnp.float32)
-    gain_two = gathered[6].astype(jnp.float32)
-    shift_two = gathered[7].astype(jnp.float32)
-    bias_qv = gathered[8].astype(jnp.float32)
-    bias_out = gathered[9].astype(jnp.float32)
-    bias_fc1 = gathered[10].astype(jnp.float32)
-    bias_fc2 = gathered[11].astype(jnp.float32)
+    whole_qkv = lax.all_gather(w_qkv, "dp", axis=0, tiled=True)
+    whole_out = lax.all_gather(w_out, "dp", axis=1, tiled=True)
+    whole_fc1 = lax.all_gather(w_fc1, "dp", axis=0, tiled=True)
+    whole_fc2 = lax.all_gather(w_fc2, "dp", axis=1, tiled=True)
+    vectors = (
+        ln1_gain,
+        ln1_bias,
+        ln2_gain,
+        ln2_bias,
+        out_bias,
+        fc2_bias,
+        fc1_bias,
+        qv_bias.reshape(-1),
+    )
+    packed = lax.all_gather(jnp.concatenate(vectors), "dp", axis=0).astype(jnp.float32)
+    wide = []
+    at = 0
+    for vector in vectors:
+        wide.append(packed[:, at : at + vector.shape[0]])
+        at += vector.shape[0]
+    gain_one, shift_one, gain_two, shift_two, bias_out, bias_fc2, bias_fc1 = (
+        part.reshape(-1) for part in wide[:7]
+    )
+    n_dp = packed.shape[0]
+    bias_qv = wide[7].reshape(n_dp, 2, -1).transpose(1, 0, 2).reshape(2, -1)
     seq_rows = tokens.shape[0]
     local_width = whole_qkv.shape[2]
     heads_here = local_width // HEAD
@@ -103,7 +100,7 @@
         .reshape(seq_rows, local_width)
     )
     attn_part = jnp.dot(mixed_heads, whole_out, preferred_element_type=jnp.float32)
-    residual = inputs + lax.psum(attn_part, "mp") + bias_out
+    residual = inputs + lax.psum(attn_part.astype(jnp.bfloat16), "mp").astype(jnp.float32) + bias_out
     normed_two = layer_norm(residual, gain_two, shift_two).astype(jnp.bfloat16)
     preact = jnp.dot(normed_two, whole_fc1, preferred_element_type=jnp.float32) + bias_fc1
     activated = smooth_gate(preact).astype(jnp.bfloat16)
@@ -133,7 +130,7 @@
         * weight_share
     )
     two_part = jnp.einsum("sf,df->sd", delta_pre_low, whole_fc1, preferred_element_type=jnp.float32)
-    delta_two = lax.psum(two_part, "mp")
+    delta_two = lax.psum(two_part.astype(jnp.bfloat16), "mp").astype(jnp.float32)
     unused_two, second_back = jax.vjp(layer_norm, residual, gain_two, shift_two)
     resid_part, gain_two_part, shift_two_part = second_back(delta_two)
     delta_resid = resid_part + grad_out
@@ -178,39 +175,46 @@
     unused_one, first_back = jax.vjp(layer_norm, inputs, gain_one, shift_one)
     input_part, gain_one_part, shift_one_part = first_back(delta_one)
     grad_tokens = input_part + delta_resid
-    stat_sums = jnp.stack(
-        [gain_two_part, shift_two_part, out_bias_part, gain_one_part, shift_one_part]
-    )
-    stat_weighted = stat_sums * weight_share
-    summed_all = (
-        lax.psum_scatter(grad_qkv, "dp", scatter_dimension=0, tiled=True),
-        lax.psum_scatter(grad_out_proj, "dp", scatter_dimension=1, tiled=True),
-        lax.psum_scatter(grad_qv, "dp", scatter_dimension=1, tiled=True),
-        lax.psum_scatter(stat_weighted[2], "dp", scatter_dimension=0, tiled=True),
-        lax.psum_scatter(stat_weighted[3], "dp", scatter_dimension=0, tiled=True),
-        lax.psum_scatter(stat_weighted[4], "dp", scatter_dimension=0, tiled=True),
-        lax.psum_scatter(grad_fc1, "dp", scatter_dimension=0, tiled=True),
-        lax.psum_scatter(grad_fc2, "dp", scatter_dimension=1, tiled=True),
-        lax.psum_scatter(grad_fc1_bias, "dp", scatter_dimension=0, tiled=True),
-        lax.psum_scatter(grad_fc2_bias, "dp", scatter_dimension=0, tiled=True),
-        lax.psum_scatter(stat_weighted[0], "dp", scatter_dimension=0, tiled=True),
-        lax.psum_scatter(stat_weighted[1], "dp", scatter_dimension=0, tiled=True),
-    )
+    grad_vectors = (
+        gain_one_part * weight_share,
+        shift_one_part * weight_share,
+        gain_two_part * weight_share,
+        shift_two_part * weight_share,
+        out_bias_part * weight_share,
+        grad_fc2_bias,
+        grad_fc1_bias,
+    )
+    stacked = jnp.concatenate(
+        [vector.reshape(n_dp, -1) for vector in grad_vectors]
+        + [grad_qv.reshape(2, n_dp, -1).transpose(1, 0, 2).reshape(n_dp, -1)],
+        axis=1,
+    )
+    own = lax.psum_scatter(stacked, "dp", scatter_dimension=0, tiled=True)[0]
+    pieces = []
+    at = 0
+    for vector in vectors:
+        pieces.append(own[at : at + vector.shape[0]])
+        at += vector.shape[0]
+
+    def scatter(grad, axis):
+        low = grad.astype(jnp.bfloat16)
+        return lax.psum_scatter(low, "dp", scatter_dimension=axis, tiled=True).astype(jnp.float32)
+
     return (
         out_tokens,
         grad_tokens,
-        summed_all[0],
-        summed_all[1],
-        summed_all[6],
-        summed_all[7],
-        summed_all[4],
-        summed_all[5],
-        summed_all[10],
-        summed_all[11],
-        summed_all[2],
-        summed_all[3],
-        summed_all[8],
-        summed_all[9],
+        scatter(grad_qkv, 0),
+        scatter(grad_out_proj, 1),
+        scatter(grad_fc1, 0),
+        scatter(grad_fc2, 1),
+        pieces[0],
+        pieces[1],
+        pieces[2],
+        pieces[3],
+        pieces[7].reshape(2, -1),
+        pieces[4],
+        pieces[6],
+        pieces[5],
     )
 
 

time: 1630 us -> 1200 us (0.74)
  waiting for transfers between devices: 1200 us -> 797 us
  blocking collectives: 96.4 us -> 36.5 us
    psum x2, waiting for transfers between devices: 527 us -> 290 us  [the longest x1 153 us: shards(): lax.psum(attn_part.astype(jnp.bfloat16), 'mp').astype(jnp.float32)]
    reduce_scatter x4, waiting for transfers between devices: 332 us -> 153 us  [scatter(): lax.psum_scatter(low, 'dp', scatter_dimension=axis, tiled=True)]
    all_gather x8 -> x1, blocking collectives: 70.9 us -> 11.2 us  [shards(): lax.all_gather(jnp.concatenate(vectors), 'dp', axis=0).astype(jnp.float32)]
    add x0 -> x1, other arithmetic: none -> 17.6 us  [shards(): grad_tokens = input_part + delta_resid]
  transfers between devices with their start and end apart: 12 -> 11, of which waited for: 9 -> 9; matrix products, arithmetic and copies ran while one was open for 12% -> 21% of each run, Pallas kernels for 0% -> 0%
where the time goes in v1:
time: 1200 us; the launch traced here: 1190 us
  waiting for transfers between devices  797 us (66%)
  matrix products  197 us (16%)
  other arithmetic  103 us (9%)
  blocking collectives  36.5 us (3%)
  local copies, waits for them, and re-layouts  35.8 us (3%)
  between operations  16.4 us (1%)
    psum x1, waiting for transfers between devices, shards(): lax.psum(ffn_part.astype(jnp.bfloat16), 'mp').astype(jnp.float32)  238 us
    reduce_scatter x4, waiting for transfers between devices, scatter(): lax.psum_scatter(low, 'dp', scatter_dimension=axis, tiled=True)  153 us
    psum x1, waiting for transfers between devices, shards(): lax.psum(attn_part.astype(jnp.bfloat16), 'mp').astype(jnp.float32)  153 us
    psum x1, waiting for transfers between devices, shards(): lax.psum(two_part.astype(jnp.bfloat16), 'mp').astype(jnp.float32)  137 us
    all_gather x1, waiting for transfers between devices, shards(): whole_fc1 = lax.all_gather(w_fc1, 'dp', axis=0, tiled=True)  46.6 us
    all_gather x1, waiting for transfers between devices, shards(): whole_fc2 = lax.all_gather(w_fc2, 'dp', axis=1, tiled=True)  41.4 us
    all_gather x1, waiting for transfers between devices, shards(): whole_qkv = lax.all_gather(w_qkv, 'dp', axis=0, tiled=True)  26.1 us
    unnamed x1, blocking collectives  25.3 us
  transfers between devices with their start and end apart: 11, of which 9 were waited for; matrix products, arithmetic and copies ran while one was open for 21% of the time, Pallas kernels for 0%

profile of v1, /device:TPU:0, one launch (start us, length us, event | category | flops | bytes accessed | tf_op | source)
XLA Modules:
  0.0 1186.2 jit_solution(16017044724826769908)
XLA Ops:
  7.2 2.3 copy.59
  17.1 11.2 all-gather.1
  29.2 2.8 convert_reduce_fusion.2
  33.9 26.1 %all-gather.7.cloned.1.call-done = bf16[2048,3,512]{0,2,1:T(8,128)(2,1)} async-done(((bf16[256,3,512]{0,2,1:T(8,128)(2,1)}), bf16[2048,3,512]{0,2,1:T(8,128)(2,1)}) %all-gather.7.cloned.1.call-update) | async-done | bytes 6291472 | tf_op jit(solution)/shard_map/all_gather | solution.py:54
  60.0 10.4 fusion.43
  72.3 7.7 fusion.62
  80.0 8.1 fusion
  90.1 7.4 divide_convert_fusion
  97.6 3.2 copy-done.6
  102.3 6.0 convolution_convert_fusion.2
  110.9 152.8 %all-reduce.6.cloned.1.call-done = bf16[1024,2048]{1,0:T(8,128)(2,1)} async-done(((bf16[1024,2048]{1,0:T(8,128)(2,1)}), bf16[1024,2048]{1,0:T(8,128)(2,1)}) %all-reduce.6.cloned.1.call-update) | async-done | bytes 4194320 | tf_op jit(solution)/shard_map/psum | solution.py:103
  263.7 5.0 fusion.26
  269.6 2.4 multiply_reduce_fusion.1
  272.0 46.6 %all-gather.11.cloned.1.call-done = bf16[2048,2048]{1,0:T(8,128)(2,1)} async-done(((bf16[256,2048]{1,0:T(8,128)(2,1)}), bf16[2048,2048]{1,0:T(8,128)(2,1)}) %all-gather.11.cloned.1.call-update) | async-done | bytes 8388624 | tf_op jit(solution)/shard_map/all_gather | solution.py:56
  318.7 16.2 %fusion.55 = f32[1024,2048]{1,0:T(8,128)} fusion(bf16[2048,2048]{1,0:T(8,128)(2,1)} %all-gather.11.cloned.1.call-done, f32[2048]{0:T(1024)S(1)} %bitcast.118, f32[2048]{0:T(1024)S(1)} %bitcast.109, f32[1024]{0:T(1024)S(1)} %fusion.48, bf16[1024,2048]{1,0:T(8,128)(2,1)} %all-reduce.6.cloned.1.call-done, bf16[1024,2048]{1,0:T(8,128)(2,1)} %param.15, ...), kind=kOutput, calls=%fused_computation.131 | convolution fusion | flops 8608808960 | bytes 25198592 | tf_op jit(solution)/shard_map/dot_general | solution.py:105
  334.8 41.4 %all-gather.13.cloned.1.call-done = bf16[2048,2048]{1,0:T(8,128)(2,1)} async-done(((bf16[2048,256]{1,0:T(8,128)(2,1)}), bf16[2048,2048]{1,0:T(8,128)(2,1)}) %all-gather.13.cloned.1.call-update) | async-done | bytes 8388624 | tf_op jit(solution)/shard_map/all_gather | solution.py:57
  376.3 20.5 %fusion.63 = (f32[2048]{0:T(1024)}, bf16[1024,2048]{1,0:T(8,128)(2,1)S(1)}) fusion(f32[1024,2048]{1,0:T(8,128)} %fusion.55, f32[2048]{0:T(1024)S(1)} %bitcast.120, bf16[2048,2048]{1,0:T(8,128)(2,1)} %all-gather.13.cloned.1.call-done, bf16[1024,2048]{1,0:T(8,128)(2,1)} %param.16, pred[1024]{0:T(1024)(128)(4,1)S(1)} %iota_compare_fusion.1), kind=kOutput, calls=%fused_computation.137 | convolution fusion | flops 8642361344 | bytes 25183232 | tf_op jit(solution)/shard_map/sd,fd->sf/dot_general | solution.py:123
  398.8 23.0 %convolution_convert_fusion = bf16[1024,2048]{1,0:T(8,128)(2,1)} fusion(bf16[2048,2048]{1,0:T(8,128)(2,1)} %all-gather.11.cloned.1.call-done, bf16[1024,2048]{1,0:T(8,128)(2,1)S(1)} %get-tuple-element.58), kind=kOutput, calls=%fused_computation.61 | convolution fusion | flops 8592031744 | bytes 16777216 | tf_op jit(solution)/shard_map/sf,df->sd/dot_general | solution.py:132
  423.2 16.6 %convolution_convert_fusion.1 = bf16[1024,2048]{1,0:T(8,128)(2,1)} fusion(bf16[2048,2048]{1,0:T(8,128)(2,1)} %all-gather.13.cloned.1.call-done, f32[1024,2048]{1,0:T(8,128)} %fusion.55, f32[2048]{0:T(1024)S(1)} %bitcast.121), kind=kOutput, calls=%fused_computation.62 | convolution fusion | flops 8613003264 | bytes 20979712 | tf_op jit(solution)/shard_map/dot_general | solution.py:107
  439.8 137.2 %all-reduce.8.cloned.1.call-done = bf16[1024,2048]{1,0:T(8,128)(2,1)} async-done(((bf16[1024,2048]{1,0:T(8,128)(2,1)}), bf16[1024,2048]{1,0:T(8,128)(2,1)}) %all-reduce.8.cloned.1.call-update) | async-done | bytes 4194320 | tf_op jit(solution)/shard_map/psum | solution.py:133
  577.0 7.6 convert_reduce_fusion.1
  585.3 5.5 fusion.21
  590.8 5.7 fusion.59
  596.5 3.2 copy-done.9
  599.7 3.7 multiply_convert_fusion.5
  603.8 6.3 fusion.39
  610.2 12.3 %multiply_reduce_fusion = (f32[4,1024]{1,0:T(4,128)S(1)}, f32[4,1024,1024]{1,2,0:T(8,128)}) fusion(f32[4,1024,1024]{1,2,0:T(8,128)} %get-tuple-element.50, f32[4,1024]{1,0:T(4,128)S(1)} %log_add_fusion, bf16[1024,4,128]{0,2,1:T(8,128)(2,1)S(1)} %bitcast.87, f32[1024,4,128]{2,0,1:T(8,128)S(1)} %copy.60, f32[4,128]{1,0:T(4,128)S(1)} %add.145), kind=kOutput, calls=%fused_computation.3 | convolution fusion | flops 1087369216 | bytes 36734976 | tf_op jit(solution)/shard_map/qhd,khd->hqk/dot_general | solution.py:149
  622.4 15.9 %multiply_convert_fusion.2 = bf16[4,1024,1024]{1,2,0:T(8,128)(2,1)} fusion(f32[4,1024,1024]{1,2,0:T(8,128)} %get-tuple-element.54, f32[4,1024,1024]{1,2,0:T(8,128)} %get-tuple-element.50, f32[4,1024]{1,0:T(4,128)S(1)} %get-tuple-element.53, f32[4,1024]{1,0:T(4,128)S(1)} %log_add_fusion), kind=kLoop, calls=%fused_computation.2 | loop fusion | flops 16777216 | bytes 41975808 | tf_op jit(solution)/shard_map/convert_element_type | solution.py:155
  638.4 4.6 bitcast_convert_fusion.1
  642.9 2.5 copy.71
  645.5 6.4 bitcast_convert_fusion.2
  651.8 2.3 copy.69
  654.1 6.3 multiply_convert_fusion.6
  660.9 11.0 bitcast_convert_fusion
  672.0 16.4 %multiply_convert_fusion = bf16[2048,2048]{1,0:T(8,128)(2,1)} fusion(f32[]{:T(128)S(6)} %div.63, bf16[1024,2048]{1,0:T(8,128)(2,1)} %param.16, pred[1024]{0:T(1024)(128)(4,1)S(1)} %iota_compare_fusion.1, f32[1024,2048]{1,0:T(8,128)} %fusion.55, f32[2048]{0:T(1024)S(1)} %bitcast.122), kind=kOutput, calls=%fused_computation | convolution fusion | flops 8625586176 | bytes 20980740 | tf_op jit(solution)/shard_map/sf,sd->fd/dot_general | solution.py:119
  689.2 15.5 %multiply_convert_fusion.1 = bf16[2048,2048]{1,0:T(8,128)(2,1)} fusion(f32[]{:T(128)S(6)} %div.63, bf16[1024,2048]{1,0:T(8,128)(2,1)} %copy-done.38, f32[2048]{0:T(1024)S(1)} %bitcast.119, f32[2048]{0:T(1024)S(1)} %bitcast.113, f32[1024]{0:T(1024)S(1)} %fusion.48, bf16[1024,2048]{1,0:T(8,128)(2,1)} %all-reduce.6.cloned.1.call-done, ...), kind=kOutput, calls=%fused_computation.1 | convolution fusion | flops 8617197568 | bytes 21004292 | tf_op jit(solution)/shard_map/sd,sf->df/dot_general | solution.py:129
  706.6 12.6 %multiply_convert_fusion.3 = bf16[2048,3,512]{2,0,1:T(8,128)(2,1)} fusion(f32[]{:T(128)S(6)} %div.63, bf16[1024,1,512]{2,0,1:T(8,128)(2,1)S(1)} %copy-done.16, bf16[1024,1,512]{2,0,1:T(8,128)(2,1)S(1)} %copy-done.19, bf16[1024,1,512]{2,0,1:T(8,128)(2,1)S(1)} %copy-done.17, bf16[1024,2048]{1,0:T(8,128)(2,1)} %param.15, f32[2048]{0:T(1024)S(1)} %bitcast.117, ...), kind=kOutput, calls=%fused_computation.9 | convolution fusion | flops 6470762496 | bytes 13656068 | tf_op jit(solution)/shard_map/sd,sce->dce/dot_general | solution.py:170
  724.0 238.4 %all-reduce.10.cloned.1.call-done = (bf16[1024,2048]{1,0:T(8,128)(2,1)}, bf16[1024,2048]{1,0:T(8,128)(2,1)}) async-done(((bf16[1024,2048]{1,0:T(8,128)(2,1)}, bf16[1024,2048]{1,0:T(8,128)(2,1)}), (bf16[1024,2048]{1,0:T(8,128)(2,1)}, bf16[1024,2048]{1,0:T(8,128)(2,1)})) %all-reduce.10.cloned.1.call-update) | async-done | bytes 8388624 | tf_op jit(solution)/shard_map/psum | solution.py:109
  962.3 5.5 convert_reduce_fusion
  968.3 4.5 fusion.22
  972.8 25.3 %all-reduce = f32[8,1920]{1,0:T(8,128)S(1)} all-reduce(f32[8,1920]{1,0:T(8,128)S(1)} %constant_dynamic-update-slice_fusion), channel_id=7, replica_groups=mesh['dp'=8,'mp'=4] {'dp'}, use_global_device_ids=true, to_apply=%region_30.31.clone | all-reduce | flops 15360 | bytes 122880
  999.5 36.7 %reduce-scatter.11.cloned.1.call-done = bf16[2048,256]{1,0:T(8,128)(2,1)} async-done(((bf16[2048,2048]{1,0:T(8,128)(2,1)}), bf16[2048,256]{1,0:T(8,128)(2,1)}) %reduce-scatter.11.cloned.1.call-update) | async-done | bytes 1048592 | tf_op jit(solution)/shard_map/reduce_scatter | solution.py:201
  1036.3 2.7 convert_element_type.148
  1039.0 72.7 %reduce-scatter.9.cloned.1.call-done = bf16[256,2048]{1,0:T(8,128)(2,1)} async-done(((bf16[2048,2048]{1,0:T(8,128)(2,1)}), bf16[256,2048]{1,0:T(8,128)(2,1)}) %reduce-scatter.9.cloned.1.call-update) | async-done | bytes 1048592 | tf_op jit(solution)/shard_map/reduce_scatter | solution.py:201
  1111.7 2.8 convert_element_type.146
  1115.8 17.6 %add_add_fusion.2 = (f32[1024,2048]{1,0:T(8,128)}, bf16[1024,2048]{1,0:T(8,128)(2,1)}) fusion(f32[1024,2048]{1,0:T(8,128)} %copy-done.9, bf16[1024,2048]{1,0:T(8,128)(2,1)} %param.15, bf16[1024,2048]{1,0:T(8,128)(2,1)} %get-tuple-element.27, f32[1024]{0:T(1024)S(1)} %negate_multiply_fusion, f32[1024]{0:T(1024)S(1)} %multiply_multiply_fusion.2, ...), kind=kLoop, calls=%fused_computation.46 | loop fusion | flops 35651584 | bytes 37789696 | tf_op jit(solution)/shard_map/add | solution.py:177
  1133.4 43.3 %reduce-scatter.5.cloned.1.call-done = bf16[256,3,512]{2,0,1:T(8,128)(2,1)} async-done(((bf16[2048,3,512]{2,0,1:T(8,128)(2,1)}), bf16[256,3,512]{2,0,1:T(8,128)(2,1)}) %reduce-scatter.5.cloned.1.call-update) | async-done | bytes 786448 | tf_op jit(solution)/shard_map/reduce_scatter | solution.py:201
  1176.7 2.5 convert_element_type.142
  (178 shorter events, 33.3 us)
Async XLA Ops:
  7.2 52.8 %all-gather.7.cloned.1.call-start = ((), (), s32[]{:S(2)}) async-start(), calls=%async_computation.4 | async-start | bytes 7077888 | tf_op jit(solution)/shard_map/all_gather | solution.py:54
  9.5 92.7 %all-gather.9.cloned.1.call-start = ((), (), s32[]{:S(2)}) async-start(), calls=%async_computation.5 | async-start | bytes 2359296 | tf_op jit(solution)/shard_map/all_gather | solution.py:55
  10.3 253.4 %all-reduce.6.cloned.1.call-start = ((), (), s32[]{:S(2)}) async-start(), calls=%async_computation.6 | async-start | bytes 8388608 | tf_op jit(solution)/shard_map/psum | solution.py:103
  17.1 14.9 %copy-start = (bf16[1024,2048]{1,0:T(8,128)(2,1)S(1)}, bf16[1024,2048]{1,0:T(8,128)(2,1)}, u32[]{:S(2)}) copy-start(bf16[1024,2048]{1,0:T(8,128)(2,1)} %param.15) | copy-start | bytes 12582916
  32.0 38.4 %copy-start.22 = (f32[1024]{0:T(1024)}, f32[1024]{0:T(1024)S(1)}, u32[]{:S(2)}) copy-start(f32[1024]{0:T(1024)S(1)} %broadcast_multiply_fusion.8) | copy-start | bytes 12292
  33.3 37.1 %copy-start.24 = (f32[1024]{0:T(1024)}, f32[1024]{0:T(1024)S(1)}, u32[]{:S(2)}) copy-start(f32[1024]{0:T(1024)S(1)} %fusion.47) | copy-start | bytes 12292
  33.6 38.7 %copy-start.29 = (f32[4,128]{1,0:T(4,128)}, f32[4,128]{1,0:T(4,128)S(1)}, u32[]{:S(2)}) copy-start(f32[4,128]{1,0:T(4,128)S(1)} %add.148) | copy-start | bytes 6148
  33.9 36.6 %copy-start.31 = (f32[1,2,8,128]{3,1,2,0:T(2,128)}, f32[1,2,8,128]{3,1,2,0:T(2,128)S(1)}, u32[]{:S(2)}) copy-start(f32[1,2,8,128]{3,1,2,0:T(2,128)S(1)} %copy.87) | copy-start | bytes 24580
  33.9 36.6 %copy-start.20 = (f32[1,2,8,128]{3,1,2,0:T(2,128)}, f32[1,2,8,128]{3,1,2,0:T(2,128)S(1)}, u32[]{:S(2)}) copy-start(f32[1,2,8,128]{3,1,2,0:T(2,128)S(1)} %copy.86) | copy-start | bytes 24580
  70.6 9.3 copy-start.12
  72.3 7.7 copy-start.10
  97.6 3.2 copy-start.6
  102.2 7.3 copy-start.36
  108.3 210.4 %all-gather.11.cloned.1.call-start = ((), (), s32[]{:S(2)}) async-start(), calls=%async_computation.7 | async-start | bytes 9437184 | tf_op jit(solution)/shard_map/all_gather | solution.py:56
  108.9 267.4 %all-gather.13.cloned.1.call-start = ((), (), s32[]{:S(2)}) async-start(), calls=%async_computation.8 | async-start | bytes 9437184 | tf_op jit(solution)/shard_map/all_gather | solution.py:57
  109.4 467.5 %all-reduce.8.cloned.1.call-start = ((), (), s32[]{:S(2)}) async-start(), calls=%async_computation.9 | async-start | bytes 8388608 | tf_op jit(solution)/shard_map/psum | solution.py:133
  109.5 209.1 %copy-start.34 = (f32[1,2,8,128]{3,1,2,0:T(2,128)}, f32[1,2,8,128]{3,1,2,0:T(2,128)S(1)}, u32[]{:S(2)}) copy-start(f32[1,2,8,128]{3,1,2,0:T(2,128)S(1)} %copy.90) | copy-start | bytes 24580
  263.6 5.0 copy-start.1
  263.7 5.9 copy-start.4
  396.8 2.0 copy-start.38
  421.8 300.4 %reduce-scatter.7.cloned.1.call-start = ((), (), s32[]{:S(2)}) async-start(), calls=%async_computation.11 | async-start | bytes 2359296 | tf_op jit(solution)/shard_map/reduce_scatter | solution.py:201
  577.0 7.7 copy-start.2
  577.0 7.7 copy-start.5
  577.0 8.3 copy-start.8
  584.6 6.2 copy-start.15
  596.5 3.2 copy-start.9
  603.3 359.0 %all-reduce.10.cloned.1.call-start = ((), (), s32[]{:S(2)}) async-start(), calls=%async_computation.14 | async-start | bytes 16777216 | tf_op jit(solution)/shard_map/psum | solution.py:109
  610.2 28.2 %slice-start = ((s8[8388608]{0:T(1024)(128)(4,1)}), s8[4194304]{0:T(1024)(128)(4,1)S(1)}, s32[]{:S(2)}) async-start(s8[8388608]{0:T(1024)(128)(4,1)} %bitcast.80), calls=%async_computation.15 | async-start | bytes 8388608
  622.4 15.9 %slice-start.1 = ((s8[8388608]{0:T(1024)(128)(4,1)}), s8[4194304]{0:T(1024)(128)(4,1)S(1)}, s32[]{:S(2)}) async-start(s8[8388608]{0:T(1024)(128)(4,1)} %bitcast.80), calls=%async_computation.16 | async-start | bytes 8388608
  638.4 7.1 copy-start.13
  642.9 11.2 copy-start.11
  642.9 11.2 copy-start.30
  660.9 11.0 copy-start.18
  672.0 364.3 %reduce-scatter.11.cloned.1.call-start = ((), (), s32[]{:S(2)}) async-start(), calls=%async_computation.13 | async-start | bytes 9437184 | tf_op jit(solution)/shard_map/reduce_scatter | solution.py:201
  688.5 423.2 %reduce-scatter.9.cloned.1.call-start = ((), (), s32[]{:S(2)}) async-start(), calls=%async_computation.12 | async-start | bytes 9437184 | tf_op jit(solution)/shard_map/reduce_scatter | solution.py:201
  704.7 1.9 copy-start.19
  704.7 1.9 copy-start.21
  704.7 1.9 copy-start.23
  704.7 1.9 copy-start.25
  704.7 1.9 copy-start.32
  704.7 14.5 %copy-start.28 = (f32[1,2,8,128]{3,2,1,0:T(8,128)S(1)}, f32[1,2,8,128]{3,2,1,0:T(8,128)}, u32[]{:S(2)}) copy-start(f32[1,2,8,128]{3,2,1,0:T(8,128)} %get-tuple-element.42) | copy-start | bytes 24580
  704.7 14.5 %copy-start.37 = (u32[32]{0:T(128)S(1)}, u32[32]{0:T(128)}, u32[]{:S(2)}) copy-start(u32[32]{0:T(128)} %constant.45) | copy-start | bytes 388
  704.8 15.1 %copy-start.33 = (f32[2048]{0:T(1024)S(1)}, f32[2048]{0:T(1024)}, u32[]{:S(2)}) copy-start(f32[2048]{0:T(1024)} %get-tuple-element.57) | copy-start | bytes 24580
  704.8 471.9 %reduce-scatter.5.cloned.1.call-start = ((), (), s32[]{:S(2)}) async-start(), calls=%async_computation.10 | async-start | bytes 7077888 | tf_op jit(solution)/shard_map/reduce_scatter | solution.py:201
  719.2 2.6 copy-start.14
  719.2 248.6 %copy-start.27 = (f32[1024]{0:T(1024)S(1)}, f32[1024]{0:T(1024)}, u32[]{:S(2)}) copy-start(f32[1024]{0:T(1024)} %copy-done.26) | copy-start | bytes 12292
  962.3 5.5 copy-start.3
  962.3 5.9 copy-start.7
  (4 other events, 4.1 us)
Sparse Core Ops, SparseCore 0:
  10.4 49.4 all-gather.6
  61.8 28.0 all-gather.8
  108.4 155.2 all-reduce.5
  265.4 53.2 all-gather.10
  320.4 55.8 all-gather.12
  422.0 154.9 all-reduce.7
  603.5 40.0 reduce-scatter.6
  672.1 290.1 all-reduce.9
  965.8 70.4 reduce-scatter.10
  1040.2 71.4 reduce-scatter.8
  1115.1 61.6 reduce-scatter.4

commit v2 on v1

--- a/solution.py
+++ b/solution.py
@@ -1,11 +1,17 @@
+import functools
 import math
 
 import jax
 import jax.numpy as jnp
 from jax import lax
+from jax.experimental import pallas as pl
+from jax.experimental.pallas import tpu as pltpu
 from jax.sharding import PartitionSpec as P
 
 HEAD = 128
+QROWS = 256
+BLOCKS = 8
+MESH = pl.DeviceIdType.MESH
 
 
 EPS = 1e-05
@@ -22,16 +28,150 @@
     return jax.nn.gelu(values, approximate=True)
 
 
-def causal_scores(queries, key_heads, inv_root):
-    row_count = queries.shape[0]
-    raw_scores = (
-        jnp.einsum("qhd,khd->hqk", queries, key_heads, preferred_element_type=jnp.float32)
-        * inv_root
-    )
-    future = lax.broadcasted_iota(jnp.int32, (row_count, row_count), 1) > lax.broadcasted_iota(
-        jnp.int32, (row_count, row_count), 0
-    )
-    return jnp.where(future[None], NEG, raw_scores)
+def future_mask(start, width, rows):
+    keys = lax.broadcasted_iota(jnp.int32, (width, rows), 0)
+    return keys > start + lax.broadcasted_iota(jnp.int32, (width, rows), 1)
+
+def attend_kernel(inv_root, q_ref, k_ref, v_ref, mixed_ref, lse_ref):
+    seq = q_ref.shape[0]
+    for start in range(0, seq, QROWS):
+        width = start + QROWS
+        scores = lax.dot_general(k_ref[:width], q_ref[start:width], (((1,), (1,)), ((), ())),
+            preferred_element_type=jnp.float32) * inv_root
+        scores = jnp.where(future_mask(start, width, QROWS), NEG, scores)
+        peak = jnp.max(scores, axis=0, keepdims=True)
+        terms = jnp.exp(scores - peak)
+        total = jnp.sum(terms, axis=0, keepdims=True)
+        lse_ref[0, :, start:width] = peak + jnp.log(total)
+        prob = (terms / total).astype(jnp.bfloat16)
+        mixed = lax.dot_general(v_ref[:width], prob, (((0,), (0,)), ((), ())), preferred_element_type=jnp.float32)
+        mixed_ref[start:width] = mixed.T.astype(jnp.bfloat16)
+
+def attend(qkv, heads):
+    seq = qkv.shape[0]
+    col = lambda c: pl.BlockSpec((seq, HEAD), lambda h, c=c: (0, c * heads + h))
+    return pl.pallas_call(
+        functools.partial(attend_kernel, 1.0 / math.sqrt(HEAD)),
+        grid=(heads,), in_specs=[col(0), col(1), col(2)],
+        out_specs=[pl.BlockSpec((seq, HEAD), lambda h: (0, h)), pl.BlockSpec((1, 1, seq), lambda h: (h, 0, 0))],
+        out_shape=[jax.ShapeDtypeStruct((seq, heads * HEAD), jnp.bfloat16), jax.ShapeDtypeStruct((heads, 1, seq), jnp.float32)],
+        name="attend")(qkv, qkv, qkv)
+
+def attend_back_kernel(inv_root, heads, q_ref, k_ref, v_ref, g_ref, lse_ref, out_ref, sums_ref, dk_acc, dv_acc):
+    seq = q_ref.shape[0]
+    head = pl.program_id(0)
+    dk_acc[...] = jnp.zeros_like(dk_acc)
+    dv_acc[...] = jnp.zeros_like(dv_acc)
+    cols = [pl.ds(pl.multiple_of((c * heads + head) * HEAD, HEAD), HEAD) for c in range(3)]
+    dq_sum = jnp.zeros((1, HEAD), jnp.float32)
+    for start in range(0, seq, QROWS):
+        width = start + QROWS
+        q = q_ref[start:width]
+        g = g_ref[start:width]
+        k = k_ref[:width]
+        nt = (((1,), (1,)), ((), ()))
+        scores = lax.dot_general(k, q, nt, preferred_element_type=jnp.float32) * inv_root
+        scores = jnp.where(future_mask(start, width, QROWS), NEG, scores)
+        prob = jnp.exp(scores - lse_ref[0, :, start:width])
+        dprob = lax.dot_general(v_ref[:width], g, nt, preferred_element_type=jnp.float32)
+        ds = (prob * (dprob - jnp.sum(prob * dprob, axis=0, keepdims=True))).astype(jnp.bfloat16)
+        dv_acc[:width] += jnp.dot(prob.astype(jnp.bfloat16), g, preferred_element_type=jnp.float32)
+        dk_acc[:width] += jnp.dot(ds, q, preferred_element_type=jnp.float32)
+        dq = lax.dot_general(k, ds, (((0,), (0,)), ((), ())), preferred_element_type=jnp.float32).T * inv_root
+        out_ref[start:width, cols[0]] = dq.astype(jnp.bfloat16)
+        dq_sum += jnp.sum(dq, axis=0, keepdims=True)
+    out_ref[:, cols[1]] = (dk_acc[...] * inv_root).astype(jnp.bfloat16)
+    dv = dv_acc[...]
+    out_ref[:, cols[2]] = dv.astype(jnp.bfloat16)
+    sums_ref[0, 0:1] = dq_sum
+    sums_ref[0, 1:2] = jnp.sum(dv, axis=0, keepdims=True)
+
+def attend_back(qkv, grad, lse, heads):
+    seq = qkv.shape[0]
+    col = lambda c: pl.BlockSpec((seq, HEAD), lambda h, c=c: (0, c * heads + h))
+    return pl.pallas_call(
+        functools.partial(attend_back_kernel, 1.0 / math.sqrt(HEAD), heads),
+        grid=(heads,), in_specs=[col(0), col(1), col(2), col(0), pl.BlockSpec((1, 1, seq), lambda h: (h, 0, 0))],
+        out_specs=[pl.BlockSpec((seq, 3 * heads * HEAD), lambda h: (0, 0)), pl.BlockSpec((1, 2, HEAD), lambda h: (h, 0, 0))],
+        out_shape=[jax.ShapeDtypeStruct((seq, 3 * heads * HEAD), jnp.bfloat16), jax.ShapeDtypeStruct((heads, 2, HEAD), jnp.float32)],
+        scratch_shapes=[pltpu.VMEM((seq, HEAD), jnp.float32)] * 2, name="attend_back")(qkv, qkv, qkv, grad, lse)
+
+
+def chain_kernel(n, blocks, x_ref, o_ref, held, s1, r1, s2, r2):
+    me = lax.axis_index("mp")
+    rows = x_ref.shape[0] // (2 * blocks)
+    right = lax.rem(me + 1, n); left = lax.rem(me + n - 1, n)
+    barrier = pltpu.get_barrier_semaphore()
+    last = n - 1
+
+    @pl.when(me > 0)
+    def _():
+        pl.semaphore_signal(barrier, inc=1, device_id={"mp": left}, device_id_type=MESH)
+
+    @pl.when(me < last)
+    def _():
+        pl.semaphore_signal(barrier, inc=1, device_id={"mp": right}, device_id_type=MESH)
+
+    pl.semaphore_wait(barrier, jnp.where(me > 0, 1, 0) + jnp.where(me < last, 1, 0))
+
+    def sl(half, b):
+        return pl.ds(pl.multiple_of((half * blocks + b) * rows, rows), rows)
+
+    def reduce_copy(half, b, src, target):
+        return pltpu.make_async_remote_copy(src_ref=src.at[sl(half, b)], dst_ref=held.at[sl(half, b)],
+            send_sem=s1.at[half * blocks + b], recv_sem=r1.at[half * blocks + b], device_id={"mp": target}, device_id_type=MESH)
+    def cast_copy(half, b, target):
+        return pltpu.make_async_remote_copy(src_ref=o_ref.at[sl(half, b)], dst_ref=o_ref.at[sl(half, b)],
+            send_sem=s2.at[half * blocks + b], recv_sem=r2.at[half * blocks + b], device_id={"mp": target}, device_id_type=MESH)
+
+    def step(t, carry):
+        for half, pos, fwd, back in ((0, me, right, left), (1, last - me, left, right)):
+            b = t - pos
+            live = jnp.logical_and(b >= 0, b < blocks)
+            @pl.when(jnp.logical_and(live, pos == 0))
+            def _():
+                reduce_copy(half, b, x_ref, fwd).start()
+            @pl.when(jnp.logical_and(live, pos > 0))
+            def _():
+                reduce_copy(half, b, x_ref, fwd).wait_recv()
+                total = held[sl(half, b)].astype(jnp.float32) + x_ref[sl(half, b)].astype(jnp.float32)
+                @pl.when(pos < last)
+                def _():
+                    held[sl(half, b)] = total.astype(jnp.bfloat16)
+                    reduce_copy(half, b, held, fwd).start()
+                @pl.when(pos == last)
+                def _():
+                    o_ref[sl(half, b)] = total.astype(jnp.bfloat16)
+                    cast_copy(half, b, back).start()
+        for half, pos, fwd, back in ((0, me, right, left), (1, last - me, left, right)):
+            b = t - (2 * last - pos)
+            live = jnp.logical_and(b >= 0, b < blocks)
+            @pl.when(jnp.logical_and(live, pos < last))
+            def _():
+                cast_copy(half, b, back).wait_recv()
+                @pl.when(pos > 0)
+                def _():
+                    cast_copy(half, b, back).start()
+        return carry
+    lax.fori_loop(0, blocks + 2 * last, step, 0)
+    def drain(b, carry):
+        for half, pos in ((0, me), (1, last - me)):
+            @pl.when(pos == 0)
+            def _(): reduce_copy(half, b, x_ref, right).wait_send()
+            @pl.when(jnp.logical_and(pos > 0, pos < last))
+            def _(): reduce_copy(half, b, held, right).wait_send()
+            @pl.when(pos > 0)
+            def _(): cast_copy(half, b, left).wait_send()
+        return carry
+    lax.fori_loop(0, blocks, drain, 0)
+
+def all_reduce(x, n, blocks, cid):
+    nb = 2 * blocks
+    vm = pl.BlockSpec(memory_space=pltpu.VMEM)
+    return pl.pallas_call(functools.partial(chain_kernel, n, blocks),
+        out_shape=jax.ShapeDtypeStruct(x.shape, x.dtype), in_specs=[vm], out_specs=vm,
+        scratch_shapes=[pltpu.VMEM(x.shape, x.dtype)] + [pltpu.SemaphoreType.DMA((nb,))] * 4,
+        compiler_params=pltpu.CompilerParams(collective_id=cid, has_side_effects=True, vmem_limit_bytes=20 << 20))(x)
 
 
 def shards(
@@ -51,7 +191,7 @@
     fc1_bias,
     fc2_bias,
 ):
-    whole_qkv = lax.all_gather(w_qkv, "dp", axis=0, tiled=True)
+    whole_qkv = lax.all_gather(w_qkv.reshape(w_qkv.shape[0], -1), "dp", axis=0, tiled=True)
     whole_out = lax.all_gather(w_out, "dp", axis=1, tiled=True)
     whole_fc1 = lax.all_gather(w_fc1, "dp", axis=0, tiled=True)
     whole_fc2 = lax.all_gather(w_fc2, "dp", axis=1, tiled=True)
@@ -75,32 +215,20 @@
         part.reshape(-1) for part in wide[:7]
     )
     n_dp = packed.shape[0]
+    n_mp = lax.axis_size("mp")
     bias_qv = wide[7].reshape(n_dp, 2, -1).transpose(1, 0, 2).reshape(2, -1)
     seq_rows = tokens.shape[0]
-    local_width = whole_qkv.shape[2]
+    local_width = w_qkv.shape[2]
     heads_here = local_width // HEAD
-    inv_root = 1.0 / math.sqrt(HEAD)
     inputs = tokens.astype(jnp.float32)
     normed_one = layer_norm(inputs, gain_one, shift_one).astype(jnp.bfloat16)
-    projected = jnp.einsum("sd,dce->sce", normed_one, whole_qkv, preferred_element_type=jnp.float32)
-    queries = (
-        (projected[:, 0] + bias_qv[0]).astype(jnp.bfloat16).reshape(seq_rows, heads_here, HEAD)
-    )
-    key_heads = projected[:, 1].astype(jnp.bfloat16).reshape(seq_rows, heads_here, HEAD)
-    values = (projected[:, 2] + bias_qv[1]).astype(jnp.bfloat16).reshape(seq_rows, heads_here, HEAD)
-    scores = causal_scores(queries, key_heads, inv_root)
-    row_peak = jnp.max(scores, axis=-1, keepdims=True)
-    exp_terms = jnp.exp(scores - row_peak)
-    exp_total = jnp.sum(exp_terms, axis=-1, keepdims=True)
-    log_total = row_peak + jnp.log(exp_total)
-    prob_low = (exp_terms / exp_total).astype(jnp.bfloat16)
-    mixed_heads = (
-        jnp.einsum("hqk,khd->qhd", prob_low, values, preferred_element_type=jnp.float32)
-        .astype(jnp.bfloat16)
-        .reshape(seq_rows, local_width)
-    )
+    bias_all = jnp.concatenate([bias_qv[0], jnp.zeros_like(bias_qv[0]), bias_qv[1]])
+    qkv = (
+        jnp.dot(normed_one, whole_qkv, preferred_element_type=jnp.float32) + bias_all
+    ).astype(jnp.bfloat16)
+    mixed_heads, log_total = attend(qkv, heads_here)
     attn_part = jnp.dot(mixed_heads, whole_out, preferred_element_type=jnp.float32)
-    residual = inputs + lax.psum(attn_part.astype(jnp.bfloat16), "mp").astype(jnp.float32) + bias_out
+    residual = inputs + all_reduce(attn_part.astype(jnp.bfloat16), n_mp, BLOCKS, 0).astype(jnp.float32) + bias_out
     normed_two = layer_norm(residual, gain_two, shift_two).astype(jnp.bfloat16)
     preact = jnp.dot(normed_two, whole_fc1, preferred_element_type=jnp.float32) + bias_fc1
     activated = smooth_gate(preact).astype(jnp.bfloat16)
@@ -130,7 +258,7 @@
         * weight_share
     )
     two_part = jnp.einsum("sf,df->sd", delta_pre_low, whole_fc1, preferred_element_type=jnp.float32)
-    delta_two = lax.psum(two_part.astype(jnp.bfloat16), "mp").astype(jnp.float32)
+    delta_two = all_reduce(two_part.astype(jnp.bfloat16), n_mp, BLOCKS, 0).astype(jnp.float32)
     unused_two, second_back = jax.vjp(layer_norm, residual, gain_two, shift_two)
     resid_part, gain_two_part, shift_two_part = second_back(delta_two)
     delta_resid = resid_part + grad_out
@@ -143,35 +271,15 @@
     delta_mixed = jnp.einsum(
         "sd,cd->sc", delta_resid_low, whole_out, preferred_element_type=jnp.float32
     )
-    delta_mixed_low = delta_mixed.astype(jnp.bfloat16).reshape(seq_rows, heads_here, HEAD)
-    scores_again = causal_scores(queries, key_heads, inv_root)
-    prob_full = jnp.exp(scores_again - log_total)
-    delta_prob = jnp.einsum(
-        "qhd,khd->hqk", delta_mixed_low, values, preferred_element_type=jnp.float32
-    )
-    delta_scores = prob_full * (
-        delta_prob - jnp.sum(prob_full * delta_prob, axis=-1, keepdims=True)
-    )
-    delta_scores_low = delta_scores.astype(jnp.bfloat16)
-    delta_q = (
-        jnp.einsum("hqk,khd->qhd", delta_scores_low, key_heads, preferred_element_type=jnp.float32)
-        * inv_root
-    ).reshape(seq_rows, local_width)
-    delta_k = (
-        jnp.einsum("hqk,qhd->khd", delta_scores_low, queries, preferred_element_type=jnp.float32)
-        * inv_root
-    ).reshape(seq_rows, local_width)
-    delta_v = jnp.einsum(
-        "hqk,qhd->khd", prob_low, delta_mixed_low, preferred_element_type=jnp.float32
-    ).reshape(seq_rows, local_width)
-    grad_qv = jnp.stack([jnp.sum(delta_q, axis=0), jnp.sum(delta_v, axis=0)]) * weight_share
-    delta_proj = jnp.stack([delta_q, delta_k, delta_v], axis=1).astype(jnp.bfloat16)
+    delta_mixed_low = delta_mixed.astype(jnp.bfloat16)
+    delta_proj, qv_sums = attend_back(qkv, delta_mixed_low, log_total, heads_here)
+    grad_qv = qv_sums.transpose(1, 0, 2).reshape(2, -1) * weight_share
     grad_qkv = (
-        jnp.einsum("sd,sce->dce", normed_one, delta_proj, preferred_element_type=jnp.float32)
+        jnp.einsum("sd,se->de", normed_one, delta_proj, preferred_element_type=jnp.float32)
         * weight_share
     )
-    one_part = jnp.einsum("sce,dce->sd", delta_proj, whole_qkv, preferred_element_type=jnp.float32)
-    delta_one = lax.psum(one_part.astype(jnp.bfloat16), "mp").astype(jnp.float32)
+    one_part = jnp.einsum("se,de->sd", delta_proj, whole_qkv, preferred_element_type=jnp.float32)
+    delta_one = all_reduce(one_part.astype(jnp.bfloat16), n_mp, BLOCKS, 0).astype(jnp.float32)
     unused_one, first_back = jax.vjp(layer_norm, inputs, gain_one, shift_one)
     input_part, gain_one_part, shift_one_part = first_back(delta_one)
     grad_tokens = input_part + delta_resid
@@ -203,7 +311,7 @@
     return (
         out_tokens,
         grad_tokens,
-        scatter(grad_qkv, 0),
+        scatter(grad_qkv, 0).reshape(w_qkv.shape),
         scatter(grad_out_proj, 1),
         scatter(grad_fc1, 0),
         scatter(grad_fc2, 1),

time: 1200 us -> 804 us (0.67)
  waiting for transfers between devices: 797 us -> 45.6 us
  Pallas kernels: 0 us -> 469 us
  matrix products: 197 us -> 146 us
  other arithmetic: 103 us -> 60.1 us
  local copies, waits for them, and re-layouts: 35.8 us -> 23 us
    pallas_call x0 -> x5, Pallas kernels: none -> 469 us  [the longest x3 446 us: all_reduce(): pl.pallas_call(functools.partial(chain_kernel, n, blocks), out_shape=jax....]
    psum x2 -> x0, waiting for transfers between devices: 290 us -> none  [the longest x1 153 us: shards(): lax.psum(attn_part.astype(jnp.bfloat16), 'mp').astype(jnp.float32)]
    psum x1, waiting for transfers between devices: 238 us -> 0.02 us  [shards(): lax.psum(ffn_part.astype(jnp.bfloat16), 'mp').astype(jnp.float32)]
    reduce_scatter x4, waiting for transfers between devices: 153 us -> 16.4 us  [scatter(): lax.psum_scatter(low, 'dp', scatter_dimension=axis, tiled=True)]
    all_gather x1, waiting for transfers between devices: 46.6 us -> 0.02 us  [shards(): whole_fc1 = lax.all_gather(w_fc1, 'dp', axis=0, tiled=True)]
    all_gather x1, waiting for transfers between devices: 41.4 us -> 0.01 us  [shards(): whole_fc2 = lax.all_gather(w_fc2, 'dp', axis=1, tiled=True)]
    dot_general x9 -> x3, matrix products: 72.6 us -> 34.1 us  [the longest x1 13 us: shards(): jnp.einsum('sd,se->de', normed_one, delta_proj, preferred_element_type=jn...]
    convert_element_type x2 -> x0, other arithmetic: 23.4 us -> none  [the longest x1 15.9 us: shards(): delta_scores_low = delta_scores.astype(jnp.bfloat16)]
  transfers between devices with their start and end apart: 11 -> 9, of which waited for: 9 -> 3; matrix products, arithmetic and copies ran while one was open for 21% -> 23% of each run, Pallas kernels for 0% -> 59%
where the time goes in v2:
time: 804 us; the launch traced here: 795 us
  Pallas kernels  469 us (58%)
  matrix products  146 us (18%)
  other arithmetic  60.1 us (7%)
  waiting for transfers between devices  45.6 us (6%)
  blocking collectives  33.8 us (4%)
  local copies, waits for them, and re-layouts  23 us (3%)
  between operations  16.2 us (2%)
    pallas_call x3, Pallas kernels, all_reduce(): pl.pallas_call(functools.partial(chain_kernel, n, blocks), out_shape=jax....  446 us
    unnamed x1, blocking collectives  22.8 us
    dot_general x1, matrix products, shards(): jnp.einsum('sd,fd->sf', grad_out_low, whole_fc2, preferred_element_type=j...  20.1 us
    all_gather x1, waiting for transfers between devices, shards(): lax.all_gather(w_qkv.reshape(w_qkv.shape[0], -1), 'dp', axis=0, tiled=True)  20 us
    reduce_sum x4, other arithmetic, layer_norm(): return center * lax.rsqrt(spread + EPS) * gain_vec + shift_vec  17.9 us
    unnamed x75, local copies, waits for them, and re-layouts  17.5 us
    reduce_scatter x4, waiting for transfers between devices, scatter(): lax.psum_scatter(low, 'dp', scatter_dimension=axis, tiled=True)  16.4 us
    dot_general x1, matrix products, shards(): jnp.einsum('sf,sd->fd', activated, grad_out_low, preferred_element_type=j...  16.3 us
  transfers between devices with their start and end apart: 9, of which 3 were waited for; matrix products, arithmetic and copies ran while one was open for 23% of the time, Pallas kernels for 59%

profile of v2, /device:TPU:0, one launch (start us, length us, event | category | flops | bytes accessed | tf_op | source)
XLA Modules:
  0.0 794.9 jit_solution(13586974602600907166)
XLA Ops:
  7.2 2.3 copy.39
  12.4 0.8 dynamic-update-slice.8
  13.2 0.8 dynamic-update-slice.9
  14.1 0.8 dynamic-update-slice.10
  14.9 0.8 dynamic-update-slice.11
  15.7 0.8 dynamic-update-slice.12
  18.4 11.0 %all-gather.1 = bf16[8,1,1920]{2,1,0:T(2,128)(2,1)S(1)} all-gather(bf16[1,1,1920]{2,1,0:T(2,128)(2,1)S(1)} %reshape.179), channel_id=2, replica_groups=mesh['dp'=8,'mp'=4] {'dp'}, dimensions={0}, use_global_device_ids=true | all-gather | bytes 34560 | tf_op jit(solution)/shard_map/all_gather | solution.py:208
  29.8 1.3 fusion.51
  33.1 2.8 convert_reduce_fusion.2
  36.0 3.4 fusion.17
  40.0 20.0 %all-gather.7.cloned.1.call-done = bf16[2048,1536]{0,1:T(8,128)(2,1)} async-done(((bf16[256,1536]{0,1:T(8,128)(2,1)}), bf16[2048,1536]{0,1:T(8,128)(2,1)}) %all-gather.7.cloned.1.call-update) | async-done | bytes 6291472 | tf_op jit(solution)/shard_map/all_gather | solution.py:194
  60.0 12.3 %add_convert_fusion.2.q_ref.k_ref.v_ref = bf16[1024,1536]{1,0:T(8,128)(2,1)} fusion(bf16[2048,1536]{0,1:T(8,128)(2,1)} %all-gather.7.cloned.1.call-done, f32[1536]{0:T(1024)S(1)} %pad_maximum_fusion, bf16[1024,2048]{1,0:T(8,128)(2,1)} %param.15, f32[2048]{0:T(1024)S(1)} %bitcast.76, f32[2048]{0:T(1024)S(1)} %bitcast.63, f32[1024]{0:T(1024)S(1)} %fusion.40, ...), kind=kOutput, calls=%fused_computation.49 | convolution fusion | flops 6458179584 | bytes 13662208 | tf_op jit(solution)/shard_map/dot_general | solution.py:227
  72.3 10.5 %attend.1 = (bf16[1024,512]{1,0:T(8,128)(2,1)}, f32[4,1,1024]{2,1,0:T(1,128)}) custom-call(bf16[1024,1536]{1,0:T(8,128)(2,1)} %add_convert_fusion.2.q_ref.k_ref.v_ref, bf16[1024,1536]{1,0:T(8,128)(2,1)} %add_convert_fusion.2.q_ref.k_ref.v_ref, bf16[1024,1536]{1,0:T(8,128)(2,1)} %add_convert_fusion.2.q_ref.k_ref.v_ref), custom_call_target="tpu_custom_call" | custom-call | tf_op jit(solution)/shard_map/attend/pallas_call | solution.py:53
  82.9 7.1 all-gather.9.cloned.1.call-done
  90.0 4.4 convolution_convert_fusion.3.x_ref
  94.4 114.0 %shard_map.254 = bf16[1024,2048]{1,0:T(8,128)(2,1)S(1)} custom-call(bf16[1024,2048]{1,0:T(8,128)(2,1)S(1)} %convolution_convert_fusion.3.x_ref), custom_call_target="tpu_custom_call" | custom-call | tf_op jit(solution)/shard_map/pallas_call | solution.py:171
  208.5 1.4 fusion.25
  209.9 2.5 multiply_reduce_fusion
  212.4 16.2 %fusion.46 = f32[1024,2048]{1,0:T(8,128)} fusion(bf16[2048,2048]{1,0:T(8,128)(2,1)} %all-gather.11.cloned.1.call-done, f32[2048]{0:T(1024)S(1)} %bitcast.81, f32[2048]{0:T(1024)S(1)} %bitcast.68, f32[1024]{0:T(1024)S(1)} %fusion.41, bf16[1024,2048]{1,0:T(8,128)(2,1)} %copy-done, bf16[1024,2048]{1,0:T(8,128)(2,1)} %param.15, ...), kind=kOutput, calls=%fused_computation.108 | convolution fusion | flops 8608808960 | bytes 25198592 | tf_op jit(solution)/shard_map/dot_general | solution.py:233
  228.6 16.0 %convolution_convert_fusion.2 = bf16[1024,2048]{1,0:T(8,128)(2,1)} fusion(bf16[2048,2048]{1,0:T(8,128)(2,1)} %all-gather.13.cloned.1.call-done, f32[1024,2048]{1,0:T(8,128)} %fusion.46, f32[2048]{0:T(1024)S(1)} %bitcast.78), kind=kOutput, calls=%fused_computation.54 | convolution fusion | flops 8613003264 | bytes 20979712 | tf_op jit(solution)/shard_map/dot_general | solution.py:235
  244.9 20.1 %fusion.54 = (f32[2048]{0:T(1024)S(1)}, bf16[1024,2048]{1,0:T(8,128)(2,1)S(1)}) fusion(f32[1024,2048]{1,0:T(8,128)} %fusion.46, f32[2048]{0:T(1024)S(1)} %bitcast.79, bf16[2048,2048]{1,0:T(8,128)(2,1)} %all-gather.13.cloned.1.call-done, bf16[1024,2048]{1,0:T(8,128)(2,1)} %param.16, pred[1024]{0:T(1024)(128)(4,1)S(1)} %iota_compare_fusion), kind=kOutput, calls=%fused_computation.112 | convolution fusion | flops 8642361344 | bytes 25183232 | tf_op jit(solution)/shard_map/sd,fd->sf/dot_general | solution.py:251
  265.0 12.8 %convolution_convert_fusion.1.x_ref = bf16[1024,2048]{1,0:T(8,128)(2,1)S(1)} fusion(bf16[2048,2048]{1,0:T(8,128)(2,1)} %all-gather.11.cloned.1.call-done, bf16[1024,2048]{1,0:T(8,128)(2,1)S(1)} %get-tuple-element.109), kind=kOutput, calls=%fused_computation.53 | convolution fusion | flops 8592031744 | bytes 16777216 | tf_op jit(solution)/shard_map/sf,df->sd/dot_general | solution.py:260
  277.9 222.3 %shard_map.255 = bf16[1024,2048]{1,0:T(8,128)(2,1)S(1)} custom-call(bf16[1024,2048]{1,0:T(8,128)(2,1)S(1)} %convolution_convert_fusion.1.x_ref), custom_call_target="tpu_custom_call" | custom-call | tf_op jit(solution)/shard_map/pallas_call | solution.py:171
  500.2 3.5 convert_reduce_fusion.1
  503.7 5.4 fusion.20
  509.2 12.8 %fusion.52 = (f32[2048]{0:T(1024)S(1)}, f32[1024,2048]{1,0:T(8,128)S(1)}, bf16[1024,2048]{1,0:T(8,128)(2,1)}, f32[2048]{0:T(1024)S(1)}) fusion(bf16[1024,2048]{1,0:T(8,128)(2,1)} %param.16, pred[1024]{0:T(1024)(128)(4,1)S(1)} %iota_compare_fusion, f32[1024]{0:T(1024)S(1)} %negate_multiply_fusion.1, f32[1024]{0:T(1024)S(1)} %multiply_multiply_fusion.3, ...), kind=kLoop, calls=%fused_computation.110 | loop fusion | flops 44036096 | bytes 33612800 | tf_op jit(solution)/shard_map/reduce_sum | solution.py:266
  522.1 3.2 copy-done.7
  525.3 3.8 multiply_convert_fusion.4
  529.3 15.4 %multiply_convert_fusion.1 = bf16[2048,2048]{1,0:T(8,128)(2,1)} fusion(f32[]{:T(128)S(6)} %div.53, bf16[1024,2048]{1,0:T(8,128)(2,1)} %copy-done.23, f32[2048]{0:T(1024)S(1)} %bitcast.82, f32[2048]{0:T(1024)S(1)} %bitcast.72, f32[1024]{0:T(1024)S(1)} %fusion.41, bf16[1024,2048]{1,0:T(8,128)(2,1)} %copy-done, bf16[1024,2048]{1,0:T(8,128)(2,1)} %param.15, ...), kind=kOutput, calls=%fused_computation.1 | convolution fusion | flops 8617197568 | bytes 21004292 | tf_op jit(solution)/shard_map/sd,sf->df/dot_general | solution.py:257
  544.8 16.3 %multiply_convert_fusion = bf16[2048,2048]{1,0:T(8,128)(2,1)} fusion(f32[]{:T(128)S(6)} %div.53, bf16[1024,2048]{1,0:T(8,128)(2,1)} %param.16, pred[1024]{0:T(1024)(128)(4,1)S(1)} %iota_compare_fusion, f32[1024,2048]{1,0:T(8,128)} %fusion.46, f32[2048]{0:T(1024)S(1)} %bitcast.80), kind=kOutput, calls=%fused_computation | convolution fusion | flops 8625586176 | bytes 20980740 | tf_op jit(solution)/shard_map/sf,sd->fd/dot_general | solution.py:247
  561.3 1.3 copy-done.21
  562.6 6.9 fusion.37.g_ref
  569.5 13.1 %attend_back.1 = (bf16[1024,1536]{1,0:T(8,128)(2,1)}, f32[4,2,128]{2,1,0:T(2,128)}) custom-call(bf16[1024,1536]{1,0:T(8,128)(2,1)} %add_convert_fusion.2.q_ref.k_ref.v_ref, bf16[1024,1536]{1,0:T(8,128)(2,1)} %add_convert_fusion.2.q_ref.k_ref.v_ref, bf16[1024,1536]{1,0:T(8,128)(2,1)} %add_convert_fusion.2.q_ref.k_ref.v_ref, bf16[1024,512]{1,0:T(8,128)(2,1)} %fusion.37.g_ref, ...), custom_call_target="tpu_custom_call" | custom-call | tf_op jit(solution)/shard_map/attend_back/pallas_call | solution.py:92
  582.7 13.0 %multiply_convert_fusion.2 = bf16[2048,1536]{1,0:T(8,128)(2,1)} fusion(bf16[1024,1536]{1,0:T(8,128)(2,1)} %get-tuple-element.20, f32[]{:T(128)S(6)} %div.53, bf16[1024,2048]{1,0:T(8,128)(2,1)} %param.15, f32[2048]{0:T(1024)S(1)} %bitcast.77, f32[2048]{0:T(1024)S(1)} %bitcast.64, f32[1024]{0:T(1024)S(1)} %copy-done.14, f32[1024]{0:T(1024)S(1)} %copy-done.12), kind=kOutput, calls=%fused_computation.2 | convolution fusion | flops 6461325312 | bytes 13656068 | tf_op jit(solution)/shard_map/sd,se->de/dot_general | solution.py:278
  596.4 8.8 %convolution_convert_fusion.x_ref = bf16[1024,2048]{1,0:T(8,128)(2,1)S(1)} fusion(bf16[1024,1536]{1,0:T(8,128)(2,1)S(1)} %copy-done.20, bf16[2048,1536]{0,1:T(8,128)(2,1)} %all-gather.7.cloned.1.call-done), kind=kOutput, calls=%fused_computation.52 | convolution fusion | flops 6444548096 | bytes 13631488 | tf_op jit(solution)/shard_map/se,de->sd/dot_general | solution.py:281
  605.2 109.3 %shard_map.256 = bf16[1024,2048]{1,0:T(8,128)(2,1)S(1)} custom-call(bf16[1024,2048]{1,0:T(8,128)(2,1)S(1)} %convolution_convert_fusion.x_ref), custom_call_target="tpu_custom_call" | custom-call | tf_op jit(solution)/shard_map/pallas_call | solution.py:171
  714.5 2.0 copy-done.2
  716.5 2.7 convert_reduce_fusion
  719.2 6.3 fusion.21
  725.9 22.8 %all-reduce = f32[8,1920]{1,0:T(8,128)S(1)} all-reduce(f32[8,1920]{1,0:T(8,128)S(1)} %constant_dynamic-update-slice_fusion), channel_id=7, replica_groups=mesh['dp'=8,'mp'=4] {'dp'}, use_global_device_ids=true, to_apply=%region_22.23.clone | all-reduce | flops 15360 | bytes 122880
  750.0 1.3 fusion.53
  751.3 9.8 %add_add_fusion.2 = f32[1024,2048]{1,0:T(8,128)} fusion(f32[1024,2048]{1,0:T(8,128)} %copy-done.7, bf16[1024,2048]{1,0:T(8,128)(2,1)} %param.15, bf16[1024,2048]{1,0:T(8,128)(2,1)} %copy-done.2, f32[1024]{0:T(1024)S(1)} %negate_multiply_fusion, f32[1024]{0:T(1024)S(1)} %multiply_multiply_fusion.2, f32[2048]{0:T(1024)S(1)} %bitcast.67, ...), kind=kLoop, calls=%fused_computation.38 | loop fusion | flops 20971520 | bytes 25190400 | tf_op jit(solution)/shard_map/add | solution.py:285
  761.2 1.8 convert_element_type.112
  763.0 2.8 convert_element_type.114
  765.8 2.7 convert_element_type.116
  768.5 16.4 %reduce-scatter.5.cloned.1.call-done = bf16[256,1536]{1,0:T(8,128)(2,1)} async-done(((bf16[2048,1536]{1,0:T(8,128)(2,1)}), bf16[256,1536]{1,0:T(8,128)(2,1)}) %reduce-scatter.5.cloned.1.call-update) | async-done | bytes 786448 | tf_op jit(solution)/shard_map/reduce_scatter | solution.py:309
  784.9 1.4 copy.40
  786.3 1.6 copy.43
  (127 shorter events, 9.5 us)
Async XLA Ops:
  7.2 52.8 %all-gather.7.cloned.1.call-start = ((), (), s32[]{:S(2)}) async-start(), calls=%async_computation.4 | async-start | bytes 7077888 | tf_op jit(solution)/shard_map/all_gather | solution.py:194
  9.5 80.5 %all-gather.9.cloned.1.call-start = ((), (), s32[]{:S(2)}) async-start(), calls=%async_computation.5 | async-start | bytes 2359296 | tf_op jit(solution)/shard_map/all_gather | solution.py:195
  10.3 202.1 %all-gather.11.cloned.1.call-start = ((), (), s32[]{:S(2)}) async-start(), calls=%async_computation.6 | async-start | bytes 9437184 | tf_op jit(solution)/shard_map/all_gather | solution.py:196
  11.0 217.6 %all-gather.13.cloned.1.call-start = ((), (), s32[]{:S(2)}) async-start(), calls=%async_computation.7 | async-start | bytes 9437184 | tf_op jit(solution)/shard_map/all_gather | solution.py:197
  11.6 497.6 %all-reduce.3.cloned.1.call-start = ((), (), s32[]{:S(2)}) async-start(), calls=%async_computation.8 | async-start | bytes 8388608 | tf_op jit(solution)/shard_map/psum | solution.py:237
  29.5 42.9 %copy-start.9 = (f32[1,2,8,128]{3,1,2,0:T(2,128)}, f32[1,2,8,128]{3,1,2,0:T(2,128)S(1)}, u32[]{:S(2)}) copy-start(f32[1,2,8,128]{3,1,2,0:T(2,128)S(1)} %copy.45) | copy-start | bytes 24580
  29.5 42.8 %copy-start.17 = (f32[1,2,8,128]{3,1,2,0:T(2,128)}, f32[1,2,8,128]{3,1,2,0:T(2,128)S(1)}, u32[]{:S(2)}) copy-start(f32[1,2,8,128]{3,1,2,0:T(2,128)S(1)} %copy.46) | copy-start | bytes 24580
  36.0 36.4 %copy-start.11 = (f32[1024]{0:T(1024)}, f32[1024]{0:T(1024)S(1)}, u32[]{:S(2)}) copy-start(f32[1024]{0:T(1024)S(1)} %broadcast_multiply_fusion.8) | copy-start | bytes 12292
  39.4 0.6 copy-start.15
  40.0 32.3 %copy-start.13 = (f32[1024]{0:T(1024)}, f32[1024]{0:T(1024)S(1)}, u32[]{:S(2)}) copy-start(f32[1024]{0:T(1024)S(1)} %fusion.40) | copy-start | bytes 12292
  90.0 118.4 %copy-start.4 = (bf16[1024,2048]{1,0:T(8,128)(2,1)S(1)}, bf16[1024,2048]{1,0:T(8,128)(2,1)}, u32[]{:S(2)}) copy-start(bf16[1024,2048]{1,0:T(8,128)(2,1)} %param.15) | copy-start | bytes 12582916
  208.4 4.0 copy-start
  244.6 516.5 %reduce-scatter.7.cloned.1.call-start = ((), (), s32[]{:S(2)}) async-start(), calls=%async_computation.10 | async-start | bytes 2359296 | tf_op jit(solution)/shard_map/reduce_scatter | solution.py:309
  265.0 12.8 %copy-start.23 = (bf16[1024,2048]{1,0:T(8,128)(2,1)}, bf16[1024,2048]{1,0:T(8,128)(2,1)S(1)}, u32[]{:S(2)}) copy-start(bf16[1024,2048]{1,0:T(8,128)(2,1)S(1)} %get-tuple-element.109) | copy-start | bytes 12582916
  277.9 222.3 %copy-start.1 = (bf16[1024,2048]{1,0:T(8,128)(2,1)S(1)}, bf16[1024,2048]{1,0:T(8,128)(2,1)}, u32[]{:S(2)}) copy-start(bf16[1024,2048]{1,0:T(8,128)(2,1)} %copy-done) | copy-start | bytes 12582916
  277.9 222.3 %copy-start.5 = (bf16[1024,2048]{1,0:T(8,128)(2,1)S(1)}, bf16[1024,2048]{1,0:T(8,128)(2,1)}, u32[]{:S(2)}) copy-start(bf16[1024,2048]{1,0:T(8,128)(2,1)} %param.15) | copy-start | bytes 12582916
  500.2 8.9 %copy-start.3 = (bf16[1024,2048]{1,0:T(8,128)(2,1)}, bf16[1024,2048]{1,0:T(8,128)(2,1)S(1)}, u32[]{:S(2)}) copy-start(bf16[1024,2048]{1,0:T(8,128)(2,1)S(1)} %shard_map.255) | copy-start | bytes 12582916
  509.2 16.1 %copy-start.8 = (bf16[1024,512]{1,0:T(8,128)(2,1)S(1)}, bf16[1024,512]{1,0:T(8,128)(2,1)}, u32[]{:S(2)}) copy-start(bf16[1024,512]{1,0:T(8,128)(2,1)} %get-tuple-element.18) | copy-start | bytes 3145732
  522.1 3.2 copy-start.7
  529.0 233.9 %reduce-scatter.9.cloned.1.call-start = ((), (), s32[]{:S(2)}) async-start(), calls=%async_computation.11 | async-start | bytes 9437184 | tf_op jit(solution)/shard_map/reduce_scatter | solution.py:309
  544.7 221.1 %reduce-scatter.11.cloned.1.call-start = ((), (), s32[]{:S(2)}) async-start(), calls=%async_computation.12 | async-start | bytes 9437184 | tf_op jit(solution)/shard_map/reduce_scatter | solution.py:309
  561.0 1.6 copy-start.21
  561.1 223.9 %reduce-scatter.5.cloned.1.call-start = ((), (), s32[]{:S(2)}) async-start(), calls=%async_computation.9 | async-start | bytes 7077888 | tf_op jit(solution)/shard_map/reduce_scatter | solution.py:309
  569.5 13.1 %copy-start.10 = (f32[1,2,8,128]{3,1,2,0:T(2,128)S(1)}, f32[1,2,8,128]{3,1,2,0:T(2,128)}, u32[]{:S(2)}) copy-start(f32[1,2,8,128]{3,1,2,0:T(2,128)} %copy-done.9) | copy-start | bytes 24580
  569.5 13.1 %copy-start.12 = (f32[1024]{0:T(1024)S(1)}, f32[1024]{0:T(1024)}, u32[]{:S(2)}) copy-start(f32[1024]{0:T(1024)} %copy-done.11) | copy-start | bytes 12292
  569.5 13.1 %copy-start.14 = (f32[1024]{0:T(1024)S(1)}, f32[1024]{0:T(1024)}, u32[]{:S(2)}) copy-start(f32[1024]{0:T(1024)} %copy-done.13) | copy-start | bytes 12292
  569.5 13.1 %copy-start.18 = (f32[1,2,8,128]{3,1,2,0:T(2,128)S(1)}, f32[1,2,8,128]{3,1,2,0:T(2,128)}, u32[]{:S(2)}) copy-start(f32[1,2,8,128]{3,1,2,0:T(2,128)} %copy-done.17) | copy-start | bytes 24580
  582.7 13.1 %copy-start.22 = (u32[32]{0:T(128)S(1)}, u32[32]{0:T(128)}, u32[]{:S(2)}) copy-start(u32[32]{0:T(128)} %constant.39) | copy-start | bytes 388
  582.7 13.7 %copy-start.20 = (bf16[1024,1536]{1,0:T(8,128)(2,1)S(1)}, bf16[1024,1536]{1,0:T(8,128)(2,1)}, u32[]{:S(2)}) copy-start(bf16[1024,1536]{1,0:T(8,128)(2,1)} %get-tuple-element.20) | copy-start | bytes 9437188
  605.2 111.3 %copy-start.6 = (bf16[1024,2048]{1,0:T(8,128)(2,1)S(1)}, bf16[1024,2048]{1,0:T(8,128)(2,1)}, u32[]{:S(2)}) copy-start(bf16[1024,2048]{1,0:T(8,128)(2,1)} %param.15) | copy-start | bytes 12582916
  605.2 114.0 %copy-start.16 = (f32[1024]{0:T(1024)S(1)}, f32[1024]{0:T(1024)}, u32[]{:S(2)}) copy-start(f32[1024]{0:T(1024)} %copy-done.15) | copy-start | bytes 12292
  714.5 2.0 copy-start.2
  716.5 9.1 %copy-start.19 = (f32[4,2,128]{2,1,0:T(2,128)S(1)}, f32[4,2,128]{2,1,0:T(2,128)}, u32[]{:S(2)}) copy-start(f32[4,2,128]{2,1,0:T(2,128)} %get-tuple-element.21) | copy-start | bytes 12292
Sparse Core Ops, SparseCore 0:
  10.4 49.5 all-gather.6
  61.9 28.0 all-gather.8
  91.9 54.2 all-gather.10
  148.0 55.8 all-gather.12
  244.8 229.5 all-reduce.2
  529.2 40.6 reduce-scatter.6
  573.3 71.5 reduce-scatter.8
  648.3 71.2 reduce-scatter.10
  723.0 61.8 reduce-scatter.4

commit v3 on v2

--- a/solution.py
+++ b/solution.py
@@ -11,6 +11,8 @@
 HEAD = 128
 QROWS = 256
 BLOCKS = 8
+SUB = 2
+VMEM_ALL = 67043328
 MESH = pl.DeviceIdType.MESH
 
 
@@ -22,10 +24,6 @@
     center = values - jnp.mean(values, axis=-1, keepdims=True)
     spread = jnp.mean(center * center, axis=-1, keepdims=True)
     return center * lax.rsqrt(spread + EPS) * gain_vec + shift_vec
-
-
-def smooth_gate(values):
-    return jax.nn.gelu(values, approximate=True)
 
 
 def future_mask(start, width, rows):
@@ -97,81 +95,560 @@
         scratch_shapes=[pltpu.VMEM((seq, HEAD), jnp.float32)] * 2, name="attend_back")(qkv, qkv, qkv, grad, lse)
 
 
-def chain_kernel(n, blocks, x_ref, o_ref, held, s1, r1, s2, r2):
+NN = (((1,), (0,)), ((), ()))
+NT = (((1,), (1,)), ((), ()))
+GELU_A = math.sqrt(2.0 / math.pi)
+GELU_B = 0.044715
+
+
+def mat(left, right, dims):
+    return lax.dot_general(left, right, dims, preferred_element_type=jnp.float32)
+
+
+class Chain:
+    def __init__(self, n, rows, part, held, total, sems):
+        self.n, self.part, self.held, self.total = n, part, held, total
+        self.s1, self.r1, self.s2, self.r2 = sems
+        self.rows = rows // (2 * BLOCKS)
+        self.me = lax.axis_index("mp")
+        self.last = n - 1
+        self.right = lax.rem(self.me + 1, n)
+        self.left = lax.rem(self.me + n - 1, n)
+        self.sides = (
+            (0, self.me, self.right, self.left),
+            (1, self.last - self.me, self.left, self.right),
+        )
+        self.steps = BLOCKS + 2 * self.last
+
+    def start_row(self, half, b):
+        return pl.multiple_of(
+            ((b // SUB) * 2 * SUB + half * SUB + b % SUB) * self.rows, self.rows
+        )
+
+    def cut(self, half, b):
+        return pl.ds(self.start_row(half, b), self.rows)
+
+    def forward(self, half, b, src, target):
+        return pltpu.make_async_remote_copy(
+            src_ref=src.at[self.cut(half, b)],
+            dst_ref=self.held.at[self.cut(half, b)],
+            send_sem=self.s1.at[half * BLOCKS + b],
+            recv_sem=self.r1.at[half * BLOCKS + b],
+            device_id={"mp": target},
+            device_id_type=MESH,
+        )
+
+    def back(self, half, b, target):
+        return pltpu.make_async_remote_copy(
+            src_ref=self.total.at[self.cut(half, b)],
+            dst_ref=self.total.at[self.cut(half, b)],
+            send_sem=self.s2.at[half * BLOCKS + b],
+            recv_sem=self.r2.at[half * BLOCKS + b],
+            device_id={"mp": target},
+            device_id_type=MESH,
+        )
+
+    def step(self, t, arrived=None):
+        for half, pos, ahead, behind in self.sides:
+            b = t - pos
+            live = jnp.logical_and(b >= 0, b < BLOCKS)
+
+            @pl.when(jnp.logical_and(live, pos == 0))
+            def _():
+                self.forward(half, b, self.part, ahead).start()
+
+            @pl.when(jnp.logical_and(live, pos > 0))
+            def _():
+                self.forward(half, b, self.part, ahead).wait_recv()
+                cut = self.cut(half, b)
+                both = self.held[cut].astype(jnp.float32) + self.part[cut].astype(jnp.float32)
+
+                @pl.when(pos < self.last)
+                def _():
+                    self.held[cut] = both.astype(jnp.bfloat16)
+                    self.forward(half, b, self.held, ahead).start()
+
+                @pl.when(pos == self.last)
+                def _():
+                    self.total[cut] = both.astype(jnp.bfloat16)
+                    self.back(half, b, behind).start()
+                    if arrived is not None:
+                        arrived(half, b, cut)
+
+        for half, pos, ahead, behind in self.sides:
+            b = t - (2 * self.last - pos)
+            live = jnp.logical_and(b >= 0, b < BLOCKS)
+
+            @pl.when(jnp.logical_and(live, pos < self.last))
+            def _():
+                self.back(half, b, behind).wait_recv()
+
+                @pl.when(pos > 0)
+                def _():
+                    self.back(half, b, behind).start()
+
+                if arrived is not None:
+                    arrived(half, b, self.cut(half, b))
+
+    def drain(self):
+        def one(b, carry):
+            for half, pos, ahead, behind in self.sides:
+
+                @pl.when(pos == 0)
+                def _():
+                    self.forward(half, b, self.part, ahead).wait_send()
+
+                @pl.when(jnp.logical_and(pos > 0, pos < self.last))
+                def _():
+                    self.forward(half, b, self.held, ahead).wait_send()
+
+                @pl.when(pos > 0)
+                def _():
+                    self.back(half, b, behind).wait_send()
+
+            return carry
+
+        lax.fori_loop(0, BLOCKS, one, 0)
+
+
+def chain_sems():
+    return [pltpu.SemaphoreType.DMA((2 * BLOCKS,))] * 4
+
+
+def greet(n):
     me = lax.axis_index("mp")
-    rows = x_ref.shape[0] // (2 * blocks)
-    right = lax.rem(me + 1, n); left = lax.rem(me + n - 1, n)
     barrier = pltpu.get_barrier_semaphore()
-    last = n - 1
 
     @pl.when(me > 0)
     def _():
-        pl.semaphore_signal(barrier, inc=1, device_id={"mp": left}, device_id_type=MESH)
-
-    @pl.when(me < last)
+        pl.semaphore_signal(
+            barrier, inc=1, device_id={"mp": lax.rem(me + n - 1, n)}, device_id_type=MESH
+        )
+
+    @pl.when(me < n - 1)
     def _():
-        pl.semaphore_signal(barrier, inc=1, device_id={"mp": right}, device_id_type=MESH)
-
-    pl.semaphore_wait(barrier, jnp.where(me > 0, 1, 0) + jnp.where(me < last, 1, 0))
-
-    def sl(half, b):
-        return pl.ds(pl.multiple_of((half * blocks + b) * rows, rows), rows)
-
-    def reduce_copy(half, b, src, target):
-        return pltpu.make_async_remote_copy(src_ref=src.at[sl(half, b)], dst_ref=held.at[sl(half, b)],
-            send_sem=s1.at[half * blocks + b], recv_sem=r1.at[half * blocks + b], device_id={"mp": target}, device_id_type=MESH)
-    def cast_copy(half, b, target):
-        return pltpu.make_async_remote_copy(src_ref=o_ref.at[sl(half, b)], dst_ref=o_ref.at[sl(half, b)],
-            send_sem=s2.at[half * blocks + b], recv_sem=r2.at[half * blocks + b], device_id={"mp": target}, device_id_type=MESH)
-
-    def step(t, carry):
-        for half, pos, fwd, back in ((0, me, right, left), (1, last - me, left, right)):
-            b = t - pos
-            live = jnp.logical_and(b >= 0, b < blocks)
-            @pl.when(jnp.logical_and(live, pos == 0))
+        pl.semaphore_signal(barrier, inc=1, device_id={"mp": lax.rem(me + 1, n)}, device_id_type=MESH)
+
+    pl.semaphore_wait(barrier, jnp.where(me > 0, 1, 0) + jnp.where(me < n - 1, 1, 0))
+
+
+def moments(wide):
+    center = wide - jnp.mean(wide, axis=-1, keepdims=True)
+    scale = lax.rsqrt(jnp.mean(center * center, axis=-1, keepdims=True) + EPS)
+    return center * scale, scale
+
+
+def ffn_kernel(
+    n, tok_hbm, att_hbm, g_hbm, w1_hbm, w2_hbm, vec_ref, b1_ref, share_ref,
+    act_hbm, low_hbm, g1_hbm, g2_hbm, sums_ref, b1sum_ref,
+    tok, att, g, w1, w2, act, dpre, nrm, part, held, total, stage, flip,
+    in_sem, w_sem, out_sem, stage_sem, s1, r1, s2, r2,
+):
+    rows, d = tok.shape
+    f = w1.shape[1]
+    group = 2 * SUB * rows // (2 * BLOCKS)
+    groups = rows // group
+    tile = 512
+    chain = Chain(n, rows, part, held, total, (s1, r1, s2, r2))
+    small = chain.rows
+
+    def load(src, dst, which, c):
+        cut = pl.ds(pl.multiple_of(c * group, group), group)
+        return pltpu.make_async_copy(src.at[cut], dst.at[cut], in_sem.at[which * groups + c])
+
+    def load_group(c):
+        load(tok_hbm, tok, 0, c).start()
+        load(att_hbm, att, 1, c).start()
+        load(g_hbm, g, 2, c).start()
+
+    load_group(0)
+    first_weight = pltpu.make_async_copy(w1_hbm, w1, w_sem.at[0])
+    second_weight = pltpu.make_async_copy(w2_hbm, w2, w_sem.at[1])
+    first_weight.start()
+    second_weight.start()
+    for c in range(1, groups):
+        load_group(c)
+    greet(n)
+    sums_ref[...] = jnp.zeros_like(sums_ref)
+    b1sum_ref[...] = jnp.zeros_like(b1sum_ref)
+    gain = vec_ref[0:1]
+    shift = vec_ref[1:2]
+    out_bias = vec_ref[2:3]
+
+    def act_out(c):
+        cut = pl.ds(pl.multiple_of(c * group, group), group)
+        return pltpu.make_async_copy(act.at[cut], act_hbm.at[cut], out_sem.at[c])
+
+    def low_out(half, b):
+        cut = chain.cut(half, b)
+        return pltpu.make_async_copy(att.at[cut], low_hbm.at[cut], out_sem.at[groups + half * BLOCKS + b])
+
+    def compute(c):
+        load(tok_hbm, tok, 0, c).wait()
+        load(att_hbm, att, 1, c).wait()
+
+        def norm(i, carry):
+            cut = pl.ds(pl.multiple_of(c * group + i * small, small), small)
+            wide = tok[cut].astype(jnp.float32) + att[cut].astype(jnp.float32) + out_bias
+            normal, _ = moments(wide)
+            nrm[cut] = (normal * gain + shift).astype(jnp.bfloat16)
+            return carry
+
+        lax.fori_loop(0, group // small, norm, 0)
+        load(g_hbm, g, 2, c).wait()
+
+    def hidden(c):
+        cut = pl.ds(pl.multiple_of(c * group, group), group)
+
+        def one(j, carry):
+            cols = pl.ds(pl.multiple_of(j * tile, tile), tile)
+            pre = mat(nrm[cut], w1[:, cols], NN) + b1_ref[:, cols]
+            square = pre * pre
+            bend = jnp.tanh(GELU_A * (pre + GELU_B * (square * pre)))
+            half_gate = 0.5 * (1.0 + bend)
+            act[cut, cols] = (pre * half_gate).astype(jnp.bfloat16)
+            slope = half_gate + 0.5 * pre * (1.0 - bend * bend) * (
+                GELU_A * (1.0 + 3.0 * GELU_B * square)
+            )
+            delta = mat(g[cut], w2[cols, :], NT) * slope
+            b1sum_ref[:, cols] += jnp.sum(delta, axis=0, keepdims=True)
+            dpre[cut, cols] = delta.astype(jnp.bfloat16)
+            return carry
+
+        lax.fori_loop(0, f // tile, one, 0)
+        act_out(c).start()
+
+        def two(j, carry):
+            cols = pl.ds(pl.multiple_of(j * tile, tile), tile)
+            part[cut, cols] = mat(dpre[cut], w1[cols, :], NT).astype(jnp.bfloat16)
+            return carry
+
+        lax.fori_loop(0, d // tile, two, 0)
+
+    def arrived(half, b, cut):
+        wide = tok[cut].astype(jnp.float32) + att[cut].astype(jnp.float32) + out_bias
+        normal, scale = moments(wide)
+        delta = total[cut].astype(jnp.float32)
+        dn = delta * gain
+        inner = dn - jnp.mean(dn, axis=-1, keepdims=True)
+        inner = inner - normal * jnp.mean(dn * normal, axis=-1, keepdims=True)
+        whole = g[cut].astype(jnp.float32) + scale * inner
+        att[cut] = whole.astype(jnp.bfloat16)
+        low_out(half, b).start()
+        sums_ref[0:1] += jnp.sum(delta * normal, axis=0, keepdims=True)
+        sums_ref[1:2] += jnp.sum(delta, axis=0, keepdims=True)
+        sums_ref[2:3] += jnp.sum(whole, axis=0, keepdims=True)
+
+    def group_step(c, carry):
+        compute(c)
+
+        @pl.when(c == 0)
+        def _():
+            first_weight.wait()
+            second_weight.wait()
+
+        hidden(c)
+        for k in range(SUB):
+            chain.step(SUB * c + k, arrived)
+        return carry
+
+    lax.fori_loop(0, groups, group_step, 0)
+
+    share = share_ref[0, 0]
+    side = 256
+    tiles_one, tiles_two = d // side, f // side
+    count = tiles_one + tiles_two
+
+    def stage_out(i):
+        slot = i % 2
+
+        def one():
+            return pltpu.make_async_copy(
+                stage.at[slot, :, pl.ds(0, f)],
+                g1_hbm.at[pl.ds(pl.multiple_of(i * side, side), side)],
+                stage_sem.at[slot],
+            )
+
+        def two():
+            return pltpu.make_async_copy(
+                stage.at[slot, :, pl.ds(0, d)],
+                g2_hbm.at[pl.ds(pl.multiple_of((i - tiles_one) * side, side), side)],
+                stage_sem.at[slot],
+            )
+
+        return one, two
+
+    def wait_stage(i):
+        one, two = stage_out(i)
+
+        @pl.when(i < tiles_one)
+        def _():
+            one().wait()
+
+        @pl.when(i >= tiles_one)
+        def _():
+            two().wait()
+
+    def grads(i):
+        slot = i % 2
+
+        @pl.when(i >= 2)
+        def _():
+            wait_stage(i - 2)
+
+        one, two = stage_out(i)
+
+        def run(left, right, width, at):
+            flip[...] = left[:, pl.ds(pl.multiple_of(at * side, side), side)].T
+
+            def tile_of(j, carry):
+                cols = pl.ds(pl.multiple_of(j * tile, tile), tile)
+                stage[slot, :, cols] = (mat(flip[...], right[:, cols], NN) * share).astype(
+                    jnp.bfloat16
+                )
+                return carry
+
+            lax.fori_loop(0, width // tile, tile_of, 0)
+
+        @pl.when(i < tiles_one)
+        def _():
+            run(nrm, dpre, f, i)
+            one().start()
+
+        @pl.when(i >= tiles_one)
+        def _():
+            run(act, g, d, i - tiles_one)
+            two().start()
+
+    extra = 2 * (n - 1)
+    each = -(-count // extra)
+
+    def tail(t, carry):
+        for k in range(each):
+            i = t * each + k
+
+            @pl.when(i < count)
             def _():
-                reduce_copy(half, b, x_ref, fwd).start()
-            @pl.when(jnp.logical_and(live, pos > 0))
-            def _():
-                reduce_copy(half, b, x_ref, fwd).wait_recv()
-                total = held[sl(half, b)].astype(jnp.float32) + x_ref[sl(half, b)].astype(jnp.float32)
-                @pl.when(pos < last)
-                def _():
-                    held[sl(half, b)] = total.astype(jnp.bfloat16)
-                    reduce_copy(half, b, held, fwd).start()
-                @pl.when(pos == last)
-                def _():
-                    o_ref[sl(half, b)] = total.astype(jnp.bfloat16)
-                    cast_copy(half, b, back).start()
-        for half, pos, fwd, back in ((0, me, right, left), (1, last - me, left, right)):
-            b = t - (2 * last - pos)
-            live = jnp.logical_and(b >= 0, b < blocks)
-            @pl.when(jnp.logical_and(live, pos < last))
-            def _():
-                cast_copy(half, b, back).wait_recv()
-                @pl.when(pos > 0)
-                def _():
-                    cast_copy(half, b, back).start()
+                grads(i)
+
+        chain.step(BLOCKS + t, arrived)
         return carry
-    lax.fori_loop(0, blocks + 2 * last, step, 0)
-    def drain(b, carry):
-        for half, pos in ((0, me), (1, last - me)):
-            @pl.when(pos == 0)
-            def _(): reduce_copy(half, b, x_ref, right).wait_send()
-            @pl.when(jnp.logical_and(pos > 0, pos < last))
-            def _(): reduce_copy(half, b, held, right).wait_send()
-            @pl.when(pos > 0)
-            def _(): cast_copy(half, b, left).wait_send()
+
+    lax.fori_loop(0, extra, tail, 0)
+    chain.drain()
+    for i in (count - 2, count - 1):
+        wait_stage(i)
+
+    def settle(b, carry):
+        for half in (0, 1):
+            low_out(half, b).wait()
         return carry
-    lax.fori_loop(0, blocks, drain, 0)
-
-def all_reduce(x, n, blocks, cid):
-    nb = 2 * blocks
+
+    lax.fori_loop(0, BLOCKS, settle, 0)
+    for c in range(groups):
+        act_out(c).wait()
+
+
+def ffn(tokens, summed, grad_low, whole_fc1, whole_fc2, vectors, bias_fc1, share, n, cid):
+    rows, d = tokens.shape
+    f = whole_fc1.shape[1]
+    groups = BLOCKS // SUB
+    anywhere = pl.BlockSpec(memory_space=pl.ANY)
     vm = pl.BlockSpec(memory_space=pltpu.VMEM)
-    return pl.pallas_call(functools.partial(chain_kernel, n, blocks),
-        out_shape=jax.ShapeDtypeStruct(x.shape, x.dtype), in_specs=[vm], out_specs=vm,
-        scratch_shapes=[pltpu.VMEM(x.shape, x.dtype)] + [pltpu.SemaphoreType.DMA((nb,))] * 4,
-        compiler_params=pltpu.CompilerParams(collective_id=cid, has_side_effects=True, vmem_limit_bytes=20 << 20))(x)
+    low = lambda *shape: pltpu.VMEM(shape, jnp.bfloat16)
+    return pl.pallas_call(
+        functools.partial(ffn_kernel, n),
+        out_shape=[
+            jax.ShapeDtypeStruct((rows, f), jnp.bfloat16),
+            jax.ShapeDtypeStruct((rows, d), jnp.bfloat16),
+            jax.ShapeDtypeStruct((d, f), jnp.bfloat16),
+            jax.ShapeDtypeStruct((f, d), jnp.bfloat16),
+            jax.ShapeDtypeStruct((3, d), jnp.float32),
+            jax.ShapeDtypeStruct((1, f), jnp.float32),
+        ],
+        in_specs=[anywhere] * 5 + [vm, vm, pl.BlockSpec(memory_space=pltpu.SMEM)],
+        out_specs=[anywhere] * 4 + [vm, vm],
+        scratch_shapes=[
+            low(rows, d), low(rows, d), low(rows, d), low(d, f), low(f, d),
+            low(rows, f), low(rows, f), low(rows, d), low(rows, d), low(rows, d), low(rows, d),
+            low(2, 256, max(d, f)), low(256, rows),
+            pltpu.SemaphoreType.DMA((3 * groups,)),
+            pltpu.SemaphoreType.DMA((2,)),
+            pltpu.SemaphoreType.DMA((groups + 2 * BLOCKS,)),
+            pltpu.SemaphoreType.DMA((2,)),
+        ] + chain_sems(),
+        compiler_params=pltpu.CompilerParams(
+            collective_id=cid, has_side_effects=True, vmem_limit_bytes=VMEM_ALL
+        ),
+        name="ffn",
+    )(tokens, summed, grad_low, whole_fc1, whole_fc2, vectors, bias_fc1, share)
+
+
+def mix_kernel(n, mixed_ref, w_ref, total, part, held, s1, r1, s2, r2):
+    rows = mixed_ref.shape[0]
+    group = SUB * rows // BLOCKS
+    chain = Chain(n, rows, part, held, total, (s1, r1, s2, r2))
+    greet(n)
+
+    def group_step(c, carry):
+        cut = pl.ds(pl.multiple_of(c * group, group), group)
+        part[cut] = mat(mixed_ref[cut], w_ref[...], NN).astype(jnp.bfloat16)
+        for k in range(SUB):
+            chain.step(SUB * c + k)
+        return carry
+
+    lax.fori_loop(0, rows // group, group_step, 0)
+    lax.fori_loop(BLOCKS, chain.steps, lambda t, carry: (chain.step(t), carry)[1], 0)
+    chain.drain()
+
+
+def mix(mixed, whole_out, n, cid):
+    rows, d = mixed.shape[0], whole_out.shape[1]
+    vm = pl.BlockSpec(memory_space=pltpu.VMEM)
+    return pl.pallas_call(
+        functools.partial(mix_kernel, n),
+        out_shape=jax.ShapeDtypeStruct((rows, d), jnp.bfloat16),
+        in_specs=[vm, vm],
+        out_specs=vm,
+        scratch_shapes=[pltpu.VMEM((rows, d), jnp.bfloat16)] * 2 + chain_sems(),
+        compiler_params=pltpu.CompilerParams(
+            collective_id=cid, has_side_effects=True, vmem_limit_bytes=28 << 20
+        ),
+        name="mix",
+    )(mixed, whole_out)
+
+
+def close_kernel(
+    n, dproj_hbm, wq_hbm, tok_hbm, low_hbm, att_hbm, act_hbm, w2_hbm, vec_ref,
+    out_hbm, gtok_hbm, sums_ref,
+    dproj, wq, tok, low, att, act, w2, part_one, held_one, total_one, part_two, held_two, total_two,
+    in_sem, out_sem, s1, r1, s2, r2, s3, r3, s4, r4,
+):
+    rows, d = tok.shape
+    f = w2.shape[0]
+    group = SUB * rows // BLOCKS
+    tile = 512
+    one = Chain(n, rows, part_one, held_one, total_one, (s1, r1, s2, r2))
+    two = Chain(n, rows, part_two, held_two, total_two, (s3, r3, s4, r4))
+    pairs = (
+        (dproj_hbm, dproj), (wq_hbm, wq), (act_hbm, act), (w2_hbm, w2),
+        (tok_hbm, tok), (att_hbm, att), (low_hbm, low),
+    )
+    loads = [pltpu.make_async_copy(a, b, in_sem.at[i]) for i, (a, b) in enumerate(pairs)]
+    for copy in loads:
+        copy.start()
+    greet(n)
+    sums_ref[...] = jnp.zeros_like(sums_ref)
+    gain = vec_ref[0:1]
+    me = lax.axis_index("mp")
+    head_flag = jnp.where(me == 0, 1.0, 0.0)
+    tail_flag = jnp.where(me == n - 1, 1.0, 0.0)
+
+    def one_out(half, b):
+        cut = one.cut(half, b)
+        return pltpu.make_async_copy(low.at[cut], gtok_hbm.at[cut], out_sem.at[half * BLOCKS + b])
+
+    def two_out(half, b):
+        cut = two.cut(half, b)
+        return pltpu.make_async_copy(
+            total_two.at[cut], out_hbm.at[cut], out_sem.at[(2 + half) * BLOCKS + b]
+        )
+
+    def arrived_one(half, b, cut):
+        normal, scale = moments(tok[cut].astype(jnp.float32))
+        delta = total_one[cut].astype(jnp.float32)
+        dn = delta * gain
+        inner = dn - jnp.mean(dn, axis=-1, keepdims=True)
+        inner = inner - normal * jnp.mean(dn * normal, axis=-1, keepdims=True)
+        low[cut] = (low[cut].astype(jnp.float32) + scale * inner).astype(jnp.bfloat16)
+        one_out(half, b).start()
+        sums_ref[0:1] += jnp.sum(delta * normal, axis=0, keepdims=True)
+        sums_ref[1:2] += jnp.sum(delta, axis=0, keepdims=True)
+
+    def arrived_two(half, b, cut):
+        two_out(half, b).start()
+
+    def group_step(c, carry):
+        cut = pl.ds(pl.multiple_of(c * group, group), group)
+
+        @pl.when(c == 0)
+        def _():
+            loads[0].wait()
+            loads[1].wait()
+
+        def first(j, carry):
+            cols = pl.ds(pl.multiple_of(j * tile, tile), tile)
+            part_one[cut, cols] = mat(dproj[cut], wq[cols, :], NT).astype(jnp.bfloat16)
+            return carry
+
+        lax.fori_loop(0, d // tile, first, 0)
+
+        @pl.when(c == 0)
+        def _():
+            for copy in loads[2:]:
+                copy.wait()
+
+        one.step(SUB * c, arrived_one)
+        half_rows = group // 2
+
+        def second(j, carry):
+            cols = pl.ds(pl.multiple_of(j * tile, tile), tile)
+            for half, flag in ((0, head_flag), (1, tail_flag)):
+                own = pl.ds(pl.multiple_of(c * group + half * half_rows, half_rows), half_rows)
+                wide = tok[own, cols].astype(jnp.float32) + att[own, cols].astype(jnp.float32)
+                part = mat(act[own], w2[:, cols], NN) + flag * (wide + vec_ref[1:2, cols])
+                part_two[own, cols] = part.astype(jnp.bfloat16)
+            return carry
+
+        lax.fori_loop(0, d // tile, second, 0)
+        for k in range(1, SUB):
+            one.step(SUB * c + k, arrived_one)
+        return carry
+
+    lax.fori_loop(0, rows // group, group_step, 0)
+
+    def later(t, carry):
+        one.step(t, arrived_one)
+        two.step(t - BLOCKS, arrived_two)
+        return carry
+
+    lax.fori_loop(BLOCKS, one.steps + BLOCKS, later, 0)
+    one.drain()
+    two.drain()
+
+    def settle(b, carry):
+        for half in (0, 1):
+            one_out(half, b).wait()
+            two_out(half, b).wait()
+        return carry
+
+    lax.fori_loop(0, BLOCKS, settle, 0)
+
+
+def close(dproj, whole_qkv, tokens, low, summed, act, whole_fc2, vectors, n, cid):
+    rows, d = tokens.shape
+    anywhere = pl.BlockSpec(memory_space=pl.ANY)
+    vm = pl.BlockSpec(memory_space=pltpu.VMEM)
+    held = [pltpu.VMEM((rows, d), jnp.bfloat16)]
+    like = lambda x: pltpu.VMEM(x.shape, jnp.bfloat16)
+    return pl.pallas_call(
+        functools.partial(close_kernel, n),
+        out_shape=[
+            jax.ShapeDtypeStruct((rows, d), jnp.bfloat16),
+            jax.ShapeDtypeStruct((rows, d), jnp.bfloat16),
+            jax.ShapeDtypeStruct((2, d), jnp.float32),
+        ],
+        in_specs=[anywhere] * 7 + [vm],
+        out_specs=[anywhere] * 2 + [vm],
+        scratch_shapes=[like(dproj), like(whole_qkv)] + held * 3 + [like(act), like(whole_fc2)]
+        + held * 6
+        + [pltpu.SemaphoreType.DMA((7,)), pltpu.SemaphoreType.DMA((4 * BLOCKS,))]
+        + chain_sems() + chain_sems(),
+        compiler_params=pltpu.CompilerParams(
+            collective_id=cid, has_side_effects=True, vmem_limit_bytes=VMEM_ALL
+        ),
+        name="close",
+    )(dproj, whole_qkv, tokens, low, summed, act, whole_fc2, vectors)
 
 
 def shards(
@@ -227,15 +704,6 @@
         jnp.dot(normed_one, whole_qkv, preferred_element_type=jnp.float32) + bias_all
     ).astype(jnp.bfloat16)
     mixed_heads, log_total = attend(qkv, heads_here)
-    attn_part = jnp.dot(mixed_heads, whole_out, preferred_element_type=jnp.float32)
-    residual = inputs + all_reduce(attn_part.astype(jnp.bfloat16), n_mp, BLOCKS, 0).astype(jnp.float32) + bias_out
-    normed_two = layer_norm(residual, gain_two, shift_two).astype(jnp.bfloat16)
-    preact = jnp.dot(normed_two, whole_fc1, preferred_element_type=jnp.float32) + bias_fc1
-    activated = smooth_gate(preact).astype(jnp.bfloat16)
-    ffn_part = jnp.dot(activated, whole_fc2, preferred_element_type=jnp.float32)
-    out_tokens = (
-        residual + lax.psum(ffn_part.astype(jnp.bfloat16), "mp").astype(jnp.float32) + bias_fc2
-    ).astype(jnp.bfloat16)
     dp_index = lax.axis_index("dp")
     slot_ids = lax.iota(jnp.int32, counts.shape[0])
     own_count = jnp.sum(jnp.where(slot_ids == dp_index, counts, 0))
@@ -243,46 +711,48 @@
     live_rows = lax.iota(jnp.int32, seq_rows) < own_count
     grad_out = jnp.where(live_rows[:, None], cotangent.astype(jnp.float32), 0.0)
     grad_out_low = grad_out.astype(jnp.bfloat16)
-    grad_fc2 = (
-        jnp.einsum("sf,sd->fd", activated, grad_out_low, preferred_element_type=jnp.float32)
-        * weight_share
-    )
     grad_fc2_bias = jnp.sum(grad_out, axis=0) * weight_share
-    delta_act = jnp.einsum("sd,fd->sf", grad_out_low, whole_fc2, preferred_element_type=jnp.float32)
-    unused_gate, gate_back = jax.vjp(smooth_gate, preact)
-    delta_pre = gate_back(delta_act)[0]
-    grad_fc1_bias = jnp.sum(delta_pre, axis=0) * weight_share
-    delta_pre_low = delta_pre.astype(jnp.bfloat16)
-    grad_fc1 = (
-        jnp.einsum("sd,sf->df", normed_two, delta_pre_low, preferred_element_type=jnp.float32)
-        * weight_share
-    )
-    two_part = jnp.einsum("sf,df->sd", delta_pre_low, whole_fc1, preferred_element_type=jnp.float32)
-    delta_two = all_reduce(two_part.astype(jnp.bfloat16), n_mp, BLOCKS, 0).astype(jnp.float32)
-    unused_two, second_back = jax.vjp(layer_norm, residual, gain_two, shift_two)
-    resid_part, gain_two_part, shift_two_part = second_back(delta_two)
-    delta_resid = resid_part + grad_out
-    delta_resid_low = delta_resid.astype(jnp.bfloat16)
-    out_bias_part = jnp.sum(delta_resid, axis=0)
+    summed = mix(mixed_heads, whole_out, n_mp, 0)
+    act, delta_resid_low, grad_fc1, grad_fc2, two_sums, fc1_sums = ffn(
+        tokens,
+        summed,
+        grad_out_low,
+        whole_fc1,
+        whole_fc2,
+        jnp.stack([gain_two, shift_two, bias_out]),
+        bias_fc1[None],
+        weight_share.reshape(1, 1),
+        n_mp,
+        1,
+    )
+    grad_fc1_bias = fc1_sums[0] * weight_share
+    delta_mixed_low = jnp.einsum(
+        "sd,cd->sc", delta_resid_low, whole_out, preferred_element_type=jnp.float32
+    ).astype(jnp.bfloat16)
     grad_out_proj = (
         jnp.einsum("sc,sd->cd", mixed_heads, delta_resid_low, preferred_element_type=jnp.float32)
         * weight_share
     )
-    delta_mixed = jnp.einsum(
-        "sd,cd->sc", delta_resid_low, whole_out, preferred_element_type=jnp.float32
-    )
-    delta_mixed_low = delta_mixed.astype(jnp.bfloat16)
     delta_proj, qv_sums = attend_back(qkv, delta_mixed_low, log_total, heads_here)
     grad_qv = qv_sums.transpose(1, 0, 2).reshape(2, -1) * weight_share
     grad_qkv = (
         jnp.einsum("sd,se->de", normed_one, delta_proj, preferred_element_type=jnp.float32)
         * weight_share
     )
-    one_part = jnp.einsum("se,de->sd", delta_proj, whole_qkv, preferred_element_type=jnp.float32)
-    delta_one = all_reduce(one_part.astype(jnp.bfloat16), n_mp, BLOCKS, 0).astype(jnp.float32)
-    unused_one, first_back = jax.vjp(layer_norm, inputs, gain_one, shift_one)
-    input_part, gain_one_part, shift_one_part = first_back(delta_one)
-    grad_tokens = input_part + delta_resid
+    out_tokens, grad_tokens, one_sums = close(
+        delta_proj,
+        whole_qkv,
+        tokens,
+        delta_resid_low,
+        summed,
+        act,
+        whole_fc2,
+        jnp.stack([gain_one, bias_out + bias_fc2]),
+        n_mp,
+        2,
+    )
+    gain_one_part, shift_one_part = one_sums[0], one_sums[1]
+    gain_two_part, shift_two_part, out_bias_part = two_sums[0], two_sums[1], two_sums[2]
     grad_vectors = (
         gain_one_part * weight_share,
         shift_one_part * weight_share,
@@ -310,7 +780,7 @@
 
     return (
         out_tokens,
-        grad_tokens,
+        grad_tokens.astype(jnp.float32),
         scatter(grad_qkv, 0).reshape(w_qkv.shape),
         scatter(grad_out_proj, 1),
         scatter(grad_fc1, 0),

time: 804 us -> 671 us (0.83)
  matrix products: 146 us -> 35.5 us
  other arithmetic: 60.1 us -> 26.3 us
  Pallas kernels: 469 us -> 494 us
  waiting for transfers between devices: 45.6 us -> 32.2 us
    dot_general x8 -> x0, matrix products: 110 us -> none  [the longest x1 20.1 us: shards(): jnp.einsum('sd,fd->sf', grad_out_low, whole_fc2, preferred_element_type=j...]
    reduce_sum x5 -> x1, other arithmetic: 30.7 us -> 3.37 us  [shards(): grad_fc2_bias = jnp.sum(grad_out, axis=0) * weight_share]
    pallas_call x3, Pallas kernels: 446 us -> 470 us  [the longest x1 214 us: close(): pl.pallas_call(functools.partial(close_kernel, n), out_shape=[jax.ShapeDt...]
    reduce_scatter x4, waiting for transfers between devices: 16.4 us -> 0.01 us  [scatter(): lax.psum_scatter(low, 'dp', scatter_dimension=axis, tiled=True)]
    add x1, other arithmetic: 9.84 us -> 0.01 us  [shards(): bias_out + bias_fc2]
    unnamed x75 -> x89, local copies, waits for them, and re-layouts: 17.5 us -> 16.9 us
  transfers between devices with their start and end apart: 9 -> 8, of which waited for: 3 -> 2; matrix products, arithmetic and copies ran while one was open for 23% -> 10% of each run, Pallas kernels for 59% -> 53%
where the time goes in v3:
time: 671 us; the launch traced here: 663 us
  Pallas kernels  494 us (74%)
  matrix products  35.5 us (5%)
  blocking collectives  33.5 us (5%)
  waiting for transfers between devices  32.2 us (5%)
  other arithmetic  26.3 us (4%)
  local copies, waits for them, and re-layouts  24.7 us (4%)
  between operations  16.5 us (2%)
    pallas_call x1, Pallas kernels, close(): pl.pallas_call(functools.partial(close_kernel, n), out_shape=[jax.ShapeDt...  214 us
    pallas_call x1, Pallas kernels, ffn(): pl.pallas_call(functools.partial(ffn_kernel, n), out_shape=[jax.ShapeDtyp...  141 us
    pallas_call x1, Pallas kernels, mix(): pl.pallas_call(functools.partial(mix_kernel, n), out_shape=jax.ShapeDtype...  115 us
    unnamed x1, blocking collectives  22.7 us
    all_gather x1, waiting for transfers between devices, shards(): lax.all_gather(w_qkv.reshape(w_qkv.shape[0], -1), 'dp', axis=0, tiled=True)  21.2 us
    unnamed x89, local copies, waits for them, and re-layouts  16.9 us
  transfers between devices with their start and end apart: 8, of which 2 were waited for; matrix products, arithmetic and copies ran while one was open for 10% of the time, Pallas kernels for 53%

profile of v3, /device:TPU:0, one launch (start us, length us, event | category | flops | bytes accessed | tf_op | source)
XLA Modules:
  0.0 662.8 jit_solution(14972904720429585869)
XLA Ops:
  7.3 1.4 copy.42
  8.7 1.2 copy.43
  10.0 0.7 all-gather.9.cloned.1.call-update
  10.7 0.7 all-gather.11.cloned.1.call-update
  12.1 0.6 fusion.11
  15.8 10.8 %all-gather.1 = bf16[8,1,1920]{2,1,0:T(2,128)(2,1)S(1)} all-gather(bf16[1,1,1920]{2,1,0:T(2,128)(2,1)S(1)} %reshape.152), channel_id=2, replica_groups=mesh['dp'=8,'mp'=4] {'dp'}, dimensions={0}, use_global_device_ids=true | all-gather | bytes 34560 | tf_op jit(solution)/shard_map/all_gather | solution.py:685
  26.9 0.6 slice_bitcast_fusion.6
  27.5 0.6 copy.54
  28.3 0.8 iota_compare_fusion
  29.1 3.2 convert_reduce_fusion
  32.4 1.2 fusion.2
  33.6 0.6 pad_maximum_fusion.vec_ref
  34.3 3.4 fusion.6
  37.6 21.2 %all-gather.7.cloned.1.call-done.wq_hbm = bf16[2048,1536]{1,0:T(8,128)(2,1)} async-done(((bf16[256,1536]{1,0:T(8,128)(2,1)}), bf16[2048,1536]{1,0:T(8,128)(2,1)}) %all-gather.7.cloned.1.call-update) | async-done | bytes 6291472 | tf_op jit(solution)/shard_map/all_gather | solution.py:671
  58.9 11.8 %add_convert_fusion.q_ref.k_ref.v_ref = bf16[1024,1536]{1,0:T(8,128)(2,1)} fusion(bf16[2048,1536]{1,0:T(8,128)(2,1)} %all-gather.7.cloned.1.call-done.wq_hbm, f32[1536]{0:T(1024)S(1)} %pad_maximum_fusion.2, bf16[1024,2048]{1,0:T(8,128)(2,1)} %tok_hbm.3, f32[2048]{0:T(1024)S(1)} %bitcast.67, f32[2048]{0:T(1024)S(1)} %bitcast.69, ...), kind=kOutput, calls=%fused_computation.12 | convolution fusion | flops 6458179584 | bytes 13662208 | tf_op jit(solution)/shard_map/dot_general | solution.py:704
  70.6 10.5 %attend.1 = (bf16[1024,512]{1,0:T(8,128)(2,1)}, f32[4,1,1024]{2,1,0:T(1,128)}) custom-call(bf16[1024,1536]{1,0:T(8,128)(2,1)} %add_convert_fusion.q_ref.k_ref.v_ref, bf16[1024,1536]{1,0:T(8,128)(2,1)} %add_convert_fusion.q_ref.k_ref.v_ref, bf16[1024,1536]{1,0:T(8,128)(2,1)} %add_convert_fusion.q_ref.k_ref.v_ref), custom_call_target="tpu_custom_call" | custom-call | tf_op jit(solution)/shard_map/attend/pallas_call | solution.py:51
  81.1 7.8 %all-gather.9.cloned.1.call-done.w_ref = bf16[512,2048]{1,0:T(8,128)(2,1)} async-done(((bf16[512,256]{1,0:T(8,128)(2,1)}), bf16[512,2048]{1,0:T(8,128)(2,1)}) %all-gather.9.cloned.1.call-update) | async-done | bytes 2097168 | tf_op jit(solution)/shard_map/all_gather | solution.py:672
  88.9 1.6 copy-done.1
  90.5 1.2 copy-done.3
  91.7 114.7 %mix.1.att_hbm = bf16[1024,2048]{1,0:T(8,128)(2,1)S(1)} custom-call(bf16[1024,512]{1,0:T(8,128)(2,1)S(1)} %copy-done.3, bf16[512,2048]{1,0:T(8,128)(2,1)S(1)} %copy-done.1), custom_call_target="tpu_custom_call" | custom-call | tf_op jit(solution)/shard_map/mix/pallas_call | solution.py:508
  206.4 2.0 copy-done
  208.4 141.0 %ffn.1 = (bf16[1024,2048]{1,0:T(8,128)(2,1)}, bf16[1024,2048]{1,0:T(8,128)(2,1)}, bf16[2048,2048]{1,0:T(8,128)(2,1)}, bf16[2048,2048]{1,0:T(8,128)(2,1)}, f32[3,2048]{1,0:T(4,128)}, /*index=5*/f32[1,2048]{1,0:T(1,128)}) custom-call(bf16[1024,2048]{1,0:T(8,128)(2,1)} %tok_hbm.3, bf16[1024,2048]{1,0:T(8,128)(2,1)} %copy-done, ...), custom_call_target="tpu_custom_call" | custom-call | tf_op jit(solution)/shard_map/ffn/pallas_call | solution.py:459
  349.5 6.3 multiply_convert_fusion.1
  355.9 5.5 convolution_convert_fusion.g_ref
  361.5 13.1 %attend_back.1 = (bf16[1024,1536]{1,0:T(8,128)(2,1)}, f32[4,2,128]{2,1,0:T(2,128)}) custom-call(bf16[1024,1536]{1,0:T(8,128)(2,1)} %add_convert_fusion.q_ref.k_ref.v_ref, bf16[1024,1536]{1,0:T(8,128)(2,1)} %add_convert_fusion.q_ref.k_ref.v_ref, bf16[1024,1536]{1,0:T(8,128)(2,1)} %add_convert_fusion.q_ref.k_ref.v_ref, ...), custom_call_target="tpu_custom_call" | custom-call | tf_op jit(solution)/shard_map/attend_back/pallas_call | solution.py:90
  374.6 11.9 %multiply_convert_fusion = bf16[2048,1536]{1,0:T(8,128)(2,1)} fusion(bf16[1024,1536]{1,0:T(8,128)(2,1)} %get-tuple-element.30.dproj_hbm, f32[]{:T(128)} %div.11, bf16[1024,2048]{1,0:T(8,128)(2,1)} %tok_hbm.3, f32[2048]{0:T(1024)S(1)} %bitcast.68, f32[2048]{0:T(1024)S(1)} %bitcast.70, f32[1024]{0:T(1024)S(1)} %copy-done.19, f32[1024]{0:T(1024)S(1)} %copy-done.12), kind=kOutput, calls=%fused_computation | convolution fusion | flops 6461325312 | bytes 13656068 | tf_op jit(solution)/shard_map/sd,se->de/dot_general | solution.py:739
  386.6 0.7 reduce-scatter.11.cloned.1.call-update
  387.4 0.6 reduce-scatter.9.cloned.1.call-update
  388.1 0.6 mul.129
  388.7 0.6 dynamic-slice
  389.4 0.6 pad_maximum_fusion.1.vec_ref
  390.0 0.6 copy.45
  390.6 214.2 %close.1 = (bf16[1024,2048]{1,0:T(8,128)(2,1)}, bf16[1024,2048]{1,0:T(8,128)(2,1)}, f32[2,2048]{1,0:T(2,128)}) custom-call(bf16[1024,1536]{1,0:T(8,128)(2,1)} %get-tuple-element.30.dproj_hbm, bf16[2048,1536]{1,0:T(8,128)(2,1)} %all-gather.7.cloned.1.call-done.wq_hbm, bf16[1024,2048]{1,0:T(8,128)(2,1)} %tok_hbm.3, ...), custom_call_target="tpu_custom_call" | custom-call | tf_op jit(solution)/shard_map/close/pallas_call | solution.py:634
  604.8 0.8 mul.135
  605.7 0.8 multiply_reduce_fusion.4
  606.6 1.0 multiply_reduce_fusion.1
  607.6 0.7 constant_dynamic-update-slice_fusion.2
  608.3 22.7 %all-reduce = f32[8,1920]{1,0:T(8,128)S(1)} all-reduce(f32[8,1920]{1,0:T(8,128)S(1)} %constant_dynamic-update-slice_fusion), channel_id=7, replica_groups=mesh['dp'=8,'mp'=4] {'dp'}, use_global_device_ids=true, to_apply=%region_9.10.clone | all-reduce | flops 15360 | bytes 122880
  631.1 0.7 dynamic-slice_reduce_fusion
  631.8 0.6 reshape.147
  632.5 6.7 %convert_element_type.55 = f32[1024,2048]{1,0:T(8,128)} convert(bf16[1024,2048]{1,0:T(8,128)(2,1)} %get-tuple-element.33) | non-fusion elementwise | flops 2097152 | bytes 12582912 | tf_op jit(solution)/shard_map/convert_element_type | solution.py:783
  639.1 1.3 fusion.12
  640.4 1.8 convert_element_type.58
  642.2 1.4 copy.44
  643.6 1.6 copy.47
  645.2 2.7 convert_element_type.60
  647.9 2.8 convert_element_type.59
  650.7 4.8 copy.75
  (121 shorter events, 3.3 us)
Async XLA Ops:
  7.2 4.9 copy-start.28
  7.2 4.9 copy-start.27
  7.2 6.9 %copy-start.20 = (bf16[256]{0:T(256)(128)(2,1)S(1)}, bf16[256]{0:T(256)(128)(2,1)}, u32[]{:S(2)}) copy-start(bf16[256]{0:T(256)(128)(2,1)} %param.22) | copy-start | bytes 1540
  7.2 7.1 %copy-start.21 = (bf16[256]{0:T(256)(128)(2,1)S(1)}, bf16[256]{0:T(256)(128)(2,1)}, u32[]{:S(2)}) copy-start(bf16[256]{0:T(256)(128)(2,1)} %param.23) | copy-start | bytes 1540
  7.2 7.3 %copy-start.22 = (bf16[256]{0:T(256)(128)(2,1)S(1)}, bf16[256]{0:T(256)(128)(2,1)}, u32[]{:S(2)}) copy-start(bf16[256]{0:T(256)(128)(2,1)} %param.24) | copy-start | bytes 1540
  7.2 7.5 %copy-start.23 = (bf16[256]{0:T(256)(128)(2,1)S(1)}, bf16[256]{0:T(256)(128)(2,1)}, u32[]{:S(2)}) copy-start(bf16[256]{0:T(256)(128)(2,1)} %param.25) | copy-start | bytes 1540
  7.2 7.7 %copy-start.24 = (bf16[256]{0:T(256)(128)(2,1)S(1)}, bf16[256]{0:T(256)(128)(2,1)}, u32[]{:S(2)}) copy-start(bf16[256]{0:T(256)(128)(2,1)} %param.27) | copy-start | bytes 1540
  7.3 7.9 %copy-start.25 = (bf16[256]{0:T(256)(128)(2,1)S(1)}, bf16[256]{0:T(256)(128)(2,1)}, u32[]{:S(2)}) copy-start(bf16[256]{0:T(256)(128)(2,1)} %param.29) | copy-start | bytes 1540
  7.3 8.1 %copy-start.26 = (bf16[256]{0:T(256)(128)(2,1)S(1)}, bf16[256]{0:T(256)(128)(2,1)}, u32[]{:S(2)}) copy-start(bf16[256]{0:T(256)(128)(2,1)} %param.28) | copy-start | bytes 1540
  7.3 51.6 %all-gather.7.cloned.1.call-start = ((), (), s32[]{:S(2)}) async-start(), calls=%async_computation.4 | async-start | bytes 7077888 | tf_op jit(solution)/shard_map/all_gather | solution.py:671
  9.9 79.0 %all-gather.9.cloned.1.call-start = ((), (), s32[]{:S(2)}) async-start(), calls=%async_computation.5 | async-start | bytes 2359296 | tf_op jit(solution)/shard_map/all_gather | solution.py:672
  10.7 197.8 %all-gather.11.cloned.1.call-start = ((), (), s32[]{:S(2)}) async-start(), calls=%async_computation.6 | async-start | bytes 9437184 | tf_op jit(solution)/shard_map/all_gather | solution.py:673
  11.4 197.0 %all-gather.13.cloned.1.call-start = ((), (), s32[]{:S(2)}) async-start(), calls=%async_computation.7 | async-start | bytes 9437184 | tf_op jit(solution)/shard_map/all_gather | solution.py:674
  12.0 628.4 %reduce-scatter.7.cloned.1.call-start = ((), (), s32[]{:S(2)}) async-start(), calls=%async_computation.9 | async-start | bytes 2359296 | tf_op jit(solution)/shard_map/reduce_scatter | solution.py:779
  28.1 5.5 copy-start.6
  28.2 30.7 %copy-start.13 = (f32[1,2,8,128]{3,1,2,0:T(2,128)}, f32[1,2,8,128]{3,1,2,0:T(2,128)S(1)}, u32[]{:S(2)}) copy-start(f32[1,2,8,128]{3,1,2,0:T(2,128)S(1)} %copy.50) | copy-start | bytes 24580
  28.2 30.7 %copy-start.15 = (f32[1,2,8,128]{3,1,2,0:T(2,128)}, f32[1,2,8,128]{3,1,2,0:T(2,128)S(1)}, u32[]{:S(2)}) copy-start(f32[1,2,8,128]{3,1,2,0:T(2,128)S(1)} %copy.49) | copy-start | bytes 24580
  28.2 4.1 copy-start.4
  29.1 5.2 copy-start.5
  32.4 26.5 %copy-start.11 = (f32[1024]{0:T(1024)}, f32[1024]{0:T(1024)S(1)}, u32[]{:S(2)}) copy-start(f32[1024]{0:T(1024)S(1)} %broadcast_multiply_fusion.1) | copy-start | bytes 12292
  33.6 25.2 %copy-start.18 = (f32[1024]{0:T(1024)}, f32[1024]{0:T(1024)S(1)}, u32[]{:S(2)}) copy-start(f32[1024]{0:T(1024)S(1)} %add_rsqrt_fusion) | copy-start | bytes 12292
  88.9 1.6 copy-start.1
  90.5 1.2 copy-start.3
  206.4 2.0 copy-start
  349.5 6.4 copy-start.2
  355.9 286.3 %reduce-scatter.5.cloned.1.call-start = ((), (), s32[]{:S(2)}) async-start(), calls=%async_computation.8 | async-start | bytes 7077888 | tf_op jit(solution)/shard_map/reduce_scatter | solution.py:779
  361.4 13.2 %copy-start.12 = (f32[1024]{0:T(1024)S(1)}, f32[1024]{0:T(1024)}, u32[]{:S(2)}) copy-start(f32[1024]{0:T(1024)} %copy-done.11) | copy-start | bytes 12292
  361.5 13.2 %copy-start.14 = (f32[1,2,8,128]{3,1,2,0:T(2,128)S(1)}, f32[1,2,8,128]{3,1,2,0:T(2,128)}, u32[]{:S(2)}) copy-start(f32[1,2,8,128]{3,1,2,0:T(2,128)} %copy-done.13) | copy-start | bytes 24580
  361.5 13.2 %copy-start.16 = (f32[1,2,8,128]{3,1,2,0:T(2,128)S(1)}, f32[1,2,8,128]{3,1,2,0:T(2,128)}, u32[]{:S(2)}) copy-start(f32[1,2,8,128]{3,1,2,0:T(2,128)} %copy-done.15) | copy-start | bytes 24580
  361.5 13.2 %copy-start.19 = (f32[1024]{0:T(1024)S(1)}, f32[1024]{0:T(1024)}, u32[]{:S(2)}) copy-start(f32[1024]{0:T(1024)} %copy-done.18) | copy-start | bytes 12292
  386.5 258.7 %reduce-scatter.11.cloned.1.call-start = ((), (), s32[]{:S(2)}) async-start(), calls=%async_computation.11 | async-start | bytes 9437184 | tf_op jit(solution)/shard_map/reduce_scatter | solution.py:779
  387.3 260.6 %reduce-scatter.9.cloned.1.call-start = ((), (), s32[]{:S(2)}) async-start(), calls=%async_computation.10 | async-start | bytes 9437184 | tf_op jit(solution)/shard_map/reduce_scatter | solution.py:779
  387.3 0.7 copy-start.10
  387.3 0.7 copy-start.9
  387.3 0.7 copy-start.7
  387.3 0.8 copy-start.8
  387.4 1.4 copy-start.29
  387.4 2.6 copy-start.17
Sparse Core Ops, SparseCore 0:
  10.5 48.2 all-gather.6
  60.7 28.1 all-gather.8
  90.8 54.2 all-gather.10
  146.8 55.8 all-gather.12
  356.0 38.4 reduce-scatter.6
  397.7 61.7 reduce-scatter.4
  463.0 71.2 reduce-scatter.10
  537.7 71.4 reduce-scatter.8

commit v4 on v3

--- a/solution.py
+++ b/solution.py
@@ -651,6 +651,263 @@
     )(dproj, whole_qkv, tokens, low, summed, act, whole_fc2, vectors)
 
 
+def greet_all(axis, n):
+    me = lax.axis_index(axis)
+    barrier = pltpu.get_barrier_semaphore()
+    for offset in range(1, n):
+        pl.semaphore_signal(
+            barrier, inc=1, device_id={axis: lax.rem(me + offset, n)}, device_id_type=MESH
+        )
+    pl.semaphore_wait(barrier, n - 1)
+
+
+def spread_kernel(n, x_ref, out_ref, got, send, recv):
+    me = lax.axis_index("dp")
+    greet_all("dp", n)
+
+    def copy(offset):
+        target = lax.rem(me + offset, n)
+        return pltpu.make_async_remote_copy(
+            src_ref=x_ref.at[target],
+            dst_ref=got.at[offset - 1],
+            send_sem=send.at[offset - 1],
+            recv_sem=recv.at[offset - 1],
+            device_id={"dp": target},
+            device_id_type=MESH,
+        )
+
+    for offset in range(1, n):
+        copy(offset).start()
+    total = x_ref[me]
+    for offset in range(1, n):
+        copy(offset).wait()
+        total = total + got[offset - 1]
+    out_ref[...] = total
+
+
+def spread(x, n, cid):
+    vm = pl.BlockSpec(memory_space=pltpu.VMEM)
+    return pl.pallas_call(
+        functools.partial(spread_kernel, n),
+        out_shape=jax.ShapeDtypeStruct(x.shape[1:], x.dtype),
+        in_specs=[vm],
+        out_specs=vm,
+        scratch_shapes=[
+            pltpu.VMEM((n - 1,) + x.shape[1:], x.dtype),
+            pltpu.SemaphoreType.DMA((n - 1,)),
+            pltpu.SemaphoreType.DMA((n - 1,)),
+        ],
+        compiler_params=pltpu.CompilerParams(
+            collective_id=cid, has_side_effects=True, vmem_limit_bytes=8 << 20
+        ),
+        name="spread",
+    )(x)
+
+
+def open_kernel(
+    n, width, own_hbm, small_ref, tok_hbm,
+    whole_hbm, nrm_hbm, qkv_hbm, packed_ref,
+    whole, tok, nrm, acc, qkv, vec, bias,
+    load_sem, out_sem, small_send, small_recv, send, recv,
+):
+    me = lax.axis_index("dp")
+    rows, d = tok.shape
+    wide = whole.shape[1]
+    shard = d // n
+    half = shard // 2
+    core = lax.rem(me, 2)
+    partner = me + 1 - 2 * core
+    along_x = me + 2 - 4 * lax.rem(me // 2, 2)
+    along_y = me + 4 - 8 * (me // 4)
+    across = along_x + along_y - me
+    partner_x = along_x + 1 - 2 * core
+    partner_y = along_y + 1 - 2 * core
+    partner_across = across + 1 - 2 * core
+
+    def piece(owner, h):
+        return pl.ds(pl.multiple_of(owner * shard + h * half, half), half)
+
+    def copy(kind, h, src, owner, target):
+        return pltpu.make_async_remote_copy(
+            src_ref=src,
+            dst_ref=whole.at[piece(owner, h)],
+            send_sem=send.at[kind * 2 + h],
+            recv_sem=recv.at[kind * 2 + h],
+            device_id={"dp": target},
+            device_id_type=MESH,
+        )
+
+    def own(kind, h, target):
+        return copy(kind, h, own_hbm.at[pl.ds(h * half, half)], me, target)
+
+    def relay(kind, h, owner, target):
+        return copy(kind, h, whole.at[piece(owner, h)], owner, target)
+
+    def arrive(kind, h, owner):
+        copy(kind, h, whole.at[piece(owner, h)], owner, partner).wait_recv()
+
+    def small_copy(offset, slot=me):
+        return pltpu.make_async_remote_copy(
+            src_ref=small_ref,
+            dst_ref=packed_ref.at[slot],
+            send_sem=small_send.at[offset - 1],
+            recv_sem=small_recv.at[offset - 1],
+            device_id={"dp": lax.rem(me + offset, n)},
+            device_id_type=MESH,
+        )
+
+    tok_load = pltpu.make_async_copy(tok_hbm, tok, load_sem.at[0])
+    tok_load.start()
+    own_load = pltpu.make_async_copy(
+        own_hbm, whole.at[pl.ds(pl.multiple_of(me * shard, shard), shard)], load_sem.at[1]
+    )
+    own_load.start()
+    greet_all("dp", n)
+    for offset in range(1, n):
+        small_copy(offset).start()
+    sends = [
+        own(0, 0, along_x), own(1, 1, along_y), own(0, 1, along_x), own(1, 0, along_y),
+        own(2, 0, partner), own(2, 1, partner),
+    ]
+    for item in sends:
+        item.start()
+    packed_ref[me] = small_ref[...]
+    for offset in range(1, n):
+        small_copy(offset, lax.rem(me + n - offset, n)).wait_recv()
+    lanes = shard // HEAD
+    for s in range(n):
+        for which in range(2):
+            for k in range(lanes):
+                at = s * shard + k * HEAD
+                vec[which : which + 1, at : at + HEAD] = packed_ref[
+                    s, which * lanes + k : which * lanes + k + 1
+                ].astype(jnp.float32)
+    local = wide // 3
+    rise = lax.broadcasted_iota(jnp.int32, (HEAD, local), 0)
+    run = lax.broadcasted_iota(jnp.int32, (HEAD, local), 1)
+    base = small_ref.shape[0] - 2
+    bias[...] = jnp.zeros_like(bias)
+    for s in range(n):
+        place = jnp.where(jnp.logical_and(run == s * width + rise, rise < width), 1.0, 0.0)
+        got = mat(packed_ref[s, base : base + 2], place.astype(jnp.bfloat16), NN)
+        bias[0:1, 0:local] += got[0:1]
+        bias[0:1, 2 * local : 3 * local] += got[1:2]
+    tok_load.wait()
+    small = 64
+
+    def norm(i, carry):
+        cut = pl.ds(pl.multiple_of(i * small, small), small)
+        normal, _ = moments(tok[cut].astype(jnp.float32))
+        nrm[cut] = (normal * vec[0:1] + vec[1:2]).astype(jnp.bfloat16)
+        return carry
+
+    lax.fori_loop(0, rows // small, norm, 0)
+    nrm_out = pltpu.make_async_copy(nrm, nrm_hbm, out_sem.at[0])
+    nrm_out.start()
+    relays = []
+
+    def pass_on(kind, h, owner, target):
+        item = relay(kind, h, owner, target)
+        item.start()
+        relays.append(item)
+
+    arrive(0, 0, along_x)
+    pass_on(3, 0, along_x, along_y)
+    pass_on(4, 0, along_x, partner)
+    arrive(1, 1, along_y)
+    pass_on(3, 1, along_y, along_x)
+    pass_on(5, 1, along_y, partner)
+    arrive(0, 1, along_x)
+    pass_on(4, 1, along_x, partner)
+    arrive(1, 0, along_y)
+    pass_on(5, 0, along_y, partner)
+    own_load.wait()
+    for h in (0, 1):
+        arrive(2, h, partner)
+        arrive(4, h, partner_x)
+        arrive(5, h, partner_y)
+    tall = rows // 2
+    tile = local
+    near = (me, partner, along_x, along_y, partner_x, partner_y)
+
+    def product_at(owners, r, cols):
+        cut = pl.ds(pl.multiple_of(r * tall, tall), tall)
+        total = None
+        for owner in owners:
+            at = pl.ds(pl.multiple_of(owner * shard, shard), shard)
+            one = mat(nrm[cut, at], whole[at, cols], NN)
+            total = one if total is None else total + one
+        return total
+
+    def early(i, carry):
+        r = i // 3
+        cols = pl.ds(pl.multiple_of(lax.rem(i, 3) * tile, tile), tile)
+        acc[pl.ds(pl.multiple_of(r * tall, tall), tall), cols] = product_at(near, r, cols)
+        return carry
+
+    lax.fori_loop(0, 6, early, 0)
+    for h in (0, 1):
+        arrive(3, h, across)
+        pass_on(6, h, across, partner)
+    for h in (0, 1):
+        arrive(6, h, partner_across)
+    whole_out = pltpu.make_async_copy(whole, whole_hbm, out_sem.at[1])
+    whole_out.start()
+
+    def late(i, carry):
+        r = i // 3
+        cut = pl.ds(pl.multiple_of(r * tall, tall), tall)
+        cols = pl.ds(pl.multiple_of(lax.rem(i, 3) * tile, tile), tile)
+        total = acc[cut, cols] + product_at((across, partner_across), r, cols)
+        qkv[cut, cols] = (total + bias[0:1, cols]).astype(jnp.bfloat16)
+        return carry
+
+    lax.fori_loop(0, 6, late, 0)
+    qkv_out = pltpu.make_async_copy(qkv, qkv_hbm, out_sem.at[2])
+    qkv_out.start()
+    for item in sends + relays:
+        item.wait_send()
+    for offset in range(1, n):
+        small_copy(offset).wait_send()
+    nrm_out.wait()
+    whole_out.wait()
+    qkv_out.wait()
+
+
+def open_layer(own, small, tokens, width, n, cid):
+    rows, d = tokens.shape
+    wide = own.shape[1]
+    anywhere = pl.BlockSpec(memory_space=pl.ANY)
+    vm = pl.BlockSpec(memory_space=pltpu.VMEM)
+    low = lambda *shape: pltpu.VMEM(shape, jnp.bfloat16)
+    full = lambda *shape: pltpu.VMEM(shape, jnp.float32)
+    return pl.pallas_call(
+        functools.partial(open_kernel, n, width),
+        out_shape=[
+            jax.ShapeDtypeStruct((d, wide), jnp.bfloat16),
+            jax.ShapeDtypeStruct((rows, d), jnp.bfloat16),
+            jax.ShapeDtypeStruct((rows, wide), jnp.bfloat16),
+            jax.ShapeDtypeStruct((n,) + small.shape, jnp.bfloat16),
+        ],
+        in_specs=[anywhere, vm, anywhere],
+        out_specs=[anywhere] * 3 + [vm],
+        scratch_shapes=[
+            low(d, wide), low(rows, d), low(rows, d), full(rows, wide), low(rows, wide),
+            full(2, d), full(1, wide),
+            pltpu.SemaphoreType.DMA((2,)),
+            pltpu.SemaphoreType.DMA((3,)),
+            pltpu.SemaphoreType.DMA((n - 1,)),
+            pltpu.SemaphoreType.DMA((n - 1,)),
+            pltpu.SemaphoreType.DMA((14,)),
+            pltpu.SemaphoreType.DMA((14,)),
+        ],
+        compiler_params=pltpu.CompilerParams(
+            collective_id=cid, has_side_effects=True, vmem_limit_bytes=40 << 20
+        ),
+        name="open",
+    )(own, small, tokens)
+
+
 def shards(
     tokens,
     cotangent,
@@ -668,7 +925,6 @@
     fc1_bias,
     fc2_bias,
 ):
-    whole_qkv = lax.all_gather(w_qkv.reshape(w_qkv.shape[0], -1), "dp", axis=0, tiled=True)
     whole_out = lax.all_gather(w_out, "dp", axis=1, tiled=True)
     whole_fc1 = lax.all_gather(w_fc1, "dp", axis=0, tiled=True)
     whole_fc2 = lax.all_gather(w_fc2, "dp", axis=1, tiled=True)
@@ -682,7 +938,26 @@
         fc1_bias,
         qv_bias.reshape(-1),
     )
-    packed = lax.all_gather(jnp.concatenate(vectors), "dp", axis=0).astype(jnp.float32)
+    n_dp = lax.axis_size("dp")
+    own_qkv = w_qkv.reshape(w_qkv.shape[0], -1)
+    fused = n_dp == 8 and w_qkv.shape[0] % (2 * HEAD) == 0
+    width = qv_bias.shape[1]
+    if fused:
+        lines = []
+        for vector in vectors[:7]:
+            lines.append(vector.reshape(-1, HEAD))
+        lines.append(jnp.pad(qv_bias, ((0, 0), (0, HEAD - width))))
+        whole_qkv, normed_one, qkv, gathered = open_layer(
+            own_qkv, jnp.concatenate(lines), tokens, width, n_dp, 4
+        )
+        flat = gathered.astype(jnp.float32).reshape(n_dp, -1)
+        packed = jnp.concatenate(
+            [flat[:, : -2 * HEAD], flat[:, -2 * HEAD : width - 2 * HEAD], flat[:, -HEAD : width - HEAD]],
+            axis=1,
+        )
+    else:
+        whole_qkv = lax.all_gather(own_qkv, "dp", axis=0, tiled=True)
+        packed = lax.all_gather(jnp.concatenate(vectors), "dp", axis=0).astype(jnp.float32)
     wide = []
     at = 0
     for vector in vectors:
@@ -691,18 +966,18 @@
     gain_one, shift_one, gain_two, shift_two, bias_out, bias_fc2, bias_fc1 = (
         part.reshape(-1) for part in wide[:7]
     )
-    n_dp = packed.shape[0]
     n_mp = lax.axis_size("mp")
     bias_qv = wide[7].reshape(n_dp, 2, -1).transpose(1, 0, 2).reshape(2, -1)
     seq_rows = tokens.shape[0]
     local_width = w_qkv.shape[2]
     heads_here = local_width // HEAD
-    inputs = tokens.astype(jnp.float32)
-    normed_one = layer_norm(inputs, gain_one, shift_one).astype(jnp.bfloat16)
-    bias_all = jnp.concatenate([bias_qv[0], jnp.zeros_like(bias_qv[0]), bias_qv[1]])
-    qkv = (
-        jnp.dot(normed_one, whole_qkv, preferred_element_type=jnp.float32) + bias_all
-    ).astype(jnp.bfloat16)
+    if not fused:
+        inputs = tokens.astype(jnp.float32)
+        normed_one = layer_norm(inputs, gain_one, shift_one).astype(jnp.bfloat16)
+        bias_all = jnp.concatenate([bias_qv[0], jnp.zeros_like(bias_qv[0]), bias_qv[1]])
+        qkv = (
+            jnp.dot(normed_one, whole_qkv, preferred_element_type=jnp.float32) + bias_all
+        ).astype(jnp.bfloat16)
     mixed_heads, log_total = attend(qkv, heads_here)
     dp_index = lax.axis_index("dp")
     slot_ids = lax.iota(jnp.int32, counts.shape[0])
@@ -767,7 +1042,9 @@
         + [grad_qv.reshape(2, n_dp, -1).transpose(1, 0, 2).reshape(n_dp, -1)],
         axis=1,
     )
-    own = lax.psum_scatter(stacked, "dp", scatter_dimension=0, tiled=True)[0]
+    length = stacked.shape[1]
+    padded = jnp.pad(stacked, ((0, 0), (0, -length % HEAD))).reshape(n_dp, -1, HEAD)
+    own = spread(padded, n_dp, 3).reshape(-1)[:length]
     pieces = []
     at = 0
     for vector in vectors:

time: 671 us -> 645 us (0.961)
  Pallas kernels: 494 us -> 546 us
  blocking collectives: 33.5 us -> 0 us
  waiting for transfers between devices: 32.2 us -> 3.27 us
  matrix products: 35.5 us -> 23.6 us
    pallas_call x0 -> x2, Pallas kernels: none -> 51.3 us  [the longest x1 45.8 us: open_layer(): pl.pallas_call(functools.partial(open_kernel, n, width), out_shape=[jax.S...]
    unnamed x1 -> x0, blocking collectives: 22.7 us -> none
    all_gather x1 -> x0, waiting for transfers between devices: 21.2 us -> none  [shards(): lax.all_gather(w_qkv.reshape(w_qkv.shape[0], -1), 'dp', axis=0, tiled=True)]
    dot_general x1 -> x0, matrix products: 11.8 us -> none  [shards(): jnp.dot(normed_one, whole_qkv, preferred_element_type=jnp.float32)]
    all_gather x1 -> x0, blocking collectives: 10.8 us -> none  [shards(): lax.all_gather(jnp.concatenate(vectors), 'dp', axis=0).astype(jnp.float32)]
    all_gather x1, waiting for transfers between devices: 7.76 us -> 0.01 us  [shards(): whole_out = lax.all_gather(w_out, 'dp', axis=1, tiled=True)]
    unnamed x89 -> x60, local copies, waits for them, and re-layouts: 16.9 us -> 19.3 us
  transfers between devices with their start and end apart: 8 -> 7, of which waited for: 2 -> 0; matrix products, arithmetic and copies ran while one was open for 10% -> 8% of each run, Pallas kernels for 53% -> 63%
where the time goes in v4:
time: 645 us; the launch traced here: 638 us
  Pallas kernels  546 us (85%)
  other arithmetic  25 us (4%)
  local copies, waits for them, and re-layouts  24.4 us (4%)
  matrix products  23.6 us (4%)
  between operations  16.2 us (3%)
    pallas_call x1, Pallas kernels, close(): pl.pallas_call(functools.partial(close_kernel, n), out_shape=[jax.ShapeDt...  214 us
    pallas_call x1, Pallas kernels, ffn(): pl.pallas_call(functools.partial(ffn_kernel, n), out_shape=[jax.ShapeDtyp...  141 us
    pallas_call x1, Pallas kernels, mix(): pl.pallas_call(functools.partial(mix_kernel, n), out_shape=jax.ShapeDtype...  115 us
    pallas_call x1, Pallas kernels, open_layer(): pl.pallas_call(functools.partial(open_kernel, n, width), out_shape=[jax.S...  45.8 us
    unnamed x60, local copies, waits for them, and re-layouts  19.3 us
    pallas_call x1, Pallas kernels, attend_back(): pl.pallas_call(functools.partial(attend_back_kernel, 1.0 / math.sqrt(HEAD...  13.1 us
  transfers between devices with their start and end apart: 7, of which 0 were waited for; matrix products, arithmetic and copies ran while one was open for 8% of the time, Pallas kernels for 63%

profile of v4, /device:TPU:0, one launch (start us, length us, event | category | flops | bytes accessed | tf_op | source)
XLA Modules:
  0.0 638.3 jit_solution(5125002080690114604)
XLA Ops:
  7.3 0.7 all-gather.4.cloned.1.call-update
  8.0 0.7 all-gather.6.cloned.1.call-update
  8.8 0.7 all-gather.8.cloned.1.call-update
  9.5 1.3 fusion.3
  12.1 1.4 copy.37
  13.5 0.3 copy.38.own_hbm
  13.9 0.1 concatenate.6.small_ref
  14.0 2.2 copy-done.2
  16.2 45.8 %open.1 = (bf16[2048,1536]{1,0:T(8,128)(2,1)}, bf16[1024,2048]{1,0:T(8,128)(2,1)S(1)}, bf16[1024,1536]{1,0:T(8,128)(2,1)S(1)}, bf16[8,16,128]{2,1,0:T(8,128)(2,1)S(1)}) custom-call(bf16[256,1536]{1,0:T(8,128)(2,1)S(1)} %copy.38.own_hbm, bf16[16,128]{1,0:T(8,128)(2,1)S(1)} %concatenate.6.small_ref, bf16[1024,2048]{1,0:T(8,128)(2,1)S(1)} %copy-done.2), custom_call_target="tpu_custom_call" | custom-call | tf_op jit(solution)/shard_map/open/pallas_call | solution.py:884
  62.0 1.7 copy-done
  63.7 2.0 copy-done.6
  65.7 0.6 slice_bitcast_fusion.1
  66.3 0.6 copy.48
  66.9 10.5 %attend.1 = (bf16[1024,512]{1,0:T(8,128)(2,1)}, f32[4,1,1024]{2,1,0:T(1,128)}) custom-call(bf16[1024,1536]{1,0:T(8,128)(2,1)} %copy-done, bf16[1024,1536]{1,0:T(8,128)(2,1)} %copy-done, bf16[1024,1536]{1,0:T(8,128)(2,1)} %copy-done), custom_call_target="tpu_custom_call" | custom-call | tf_op jit(solution)/shard_map/attend/pallas_call | solution.py:51
  77.5 0.7 iota_compare_fusion
  78.2 0.6 pad_maximum_fusion.vec_ref
  78.8 6.0 fusion
  84.9 1.6 copy-done.3
  86.5 115.3 %mix.1.att_hbm = bf16[1024,2048]{1,0:T(8,128)(2,1)S(1)} custom-call(bf16[1024,512]{1,0:T(8,128)(2,1)S(1)} %copy-done.5, bf16[512,2048]{1,0:T(8,128)(2,1)S(1)} %copy-done.3), custom_call_target="tpu_custom_call" | custom-call | tf_op jit(solution)/shard_map/mix/pallas_call | solution.py:508
  201.8 2.0 copy-done.1
  203.8 141.2 %ffn.1 = (bf16[1024,2048]{1,0:T(8,128)(2,1)}, bf16[1024,2048]{1,0:T(8,128)(2,1)}, bf16[2048,2048]{1,0:T(8,128)(2,1)}, bf16[2048,2048]{1,0:T(8,128)(2,1)}, f32[3,2048]{1,0:T(4,128)}, /*index=5*/f32[1,2048]{1,0:T(1,128)}) custom-call(bf16[1024,2048]{1,0:T(8,128)(2,1)} %tok_hbm.5, bf16[1024,2048]{1,0:T(8,128)(2,1)} %copy-done.1, ...), custom_call_target="tpu_custom_call" | custom-call | tf_op jit(solution)/shard_map/ffn/pallas_call | solution.py:459
  345.1 6.3 multiply_convert_fusion.1
  351.4 0.0 reduce-scatter.5.cloned.1.call-start
  351.5 5.5 convolution_convert_fusion.g_ref
  357.0 13.1 %attend_back.1 = (bf16[1024,1536]{1,0:T(8,128)(2,1)}, f32[4,2,128]{2,1,0:T(2,128)}) custom-call(bf16[1024,1536]{1,0:T(8,128)(2,1)} %copy-done, bf16[1024,1536]{1,0:T(8,128)(2,1)} %copy-done, bf16[1024,1536]{1,0:T(8,128)(2,1)} %copy-done, bf16[1024,512]{1,0:T(8,128)(2,1)} %convolution_convert_fusion.g_ref, f32[4,1,1024]{2,1,0:T(1,128)} %get-tuple-element.35.lse_ref), custom_call_target="tpu_custom_call" | custom-call | tf_op jit(solution)/shard_map/attend_back/pallas_call | solution.py:90
  370.1 11.7 %multiply_convert_fusion = bf16[2048,1536]{1,0:T(8,128)(2,1)} fusion(bf16[1024,2048]{1,0:T(8,128)(2,1)} %copy-done.6, bf16[1024,1536]{1,0:T(8,128)(2,1)} %get-tuple-element.36.dproj_hbm, f32[]{:T(128)} %div.3), kind=kOutput, calls=%fused_computation | convolution fusion | flops 6448742400 | bytes 13631492 | tf_op jit(solution)/shard_map/sd,se->de/dot_general | solution.py:1014
  381.9 0.0 reduce-scatter.11.cloned.1.call-start
  381.9 0.5 reduce-scatter.11.cloned.1.call-update
  382.5 0.6 reduce-scatter.9.cloned.1.call-update
  383.2 0.6 mul.102
  383.9 0.6 pad_maximum_fusion.1.vec_ref
  384.5 0.6 copy.40
  385.1 214.0 %close.1 = (bf16[1024,2048]{1,0:T(8,128)(2,1)}, bf16[1024,2048]{1,0:T(8,128)(2,1)}, f32[2,2048]{1,0:T(2,128)}) custom-call(bf16[1024,1536]{1,0:T(8,128)(2,1)} %get-tuple-element.36.dproj_hbm, bf16[2048,1536]{1,0:T(8,128)(2,1)} %get-tuple-element.37.wq_hbm, bf16[1024,2048]{1,0:T(8,128)(2,1)} %tok_hbm.5, bf16[1024,2048]{1,0:T(8,128)(2,1)} %get-tuple-element.34.low_hbm, ...), custom_call_target="tpu_custom_call" | custom-call | tf_op jit(solution)/shard_map/close/pallas_call | solution.py:634
  599.1 0.8 mul.108
  599.9 0.1 reshape.158
  600.0 1.0 multiply_reduce_fusion.1
  601.0 0.8 multiply_reduce_fusion.4
  601.9 0.7 constant_dynamic-update-slice_fusion.2
  602.7 5.5 spread.1
  608.2 0.6 reshape.160
  608.9 6.7 %convert_element_type.42 = f32[1024,2048]{1,0:T(8,128)} convert(bf16[1024,2048]{1,0:T(8,128)(2,1)} %get-tuple-element.40) | non-fusion elementwise | flops 2097152 | bytes 12582912 | tf_op jit(solution)/shard_map/convert_element_type | solution.py:1060
  615.5 0.6 slice_bitcast_fusion.6
  616.1 1.8 convert_element_type.45
  617.9 1.4 copy.39
  619.3 1.6 copy.43
  620.9 2.7 convert_element_type.47
  623.6 2.8 convert_element_type.46
  626.4 4.8 copy.61
  (78 shorter events, 0.5 us)
Async XLA Ops:
  7.2 6.6 %copy-start.20 = (bf16[2,64]{1,0:T(2,128)(2,1)S(1)}, bf16[2,64]{1,0:T(2,128)(2,1)}, u32[]{:S(2)}) copy-start(bf16[2,64]{1,0:T(2,128)(2,1)} %param.26) | copy-start | bytes 772
  7.2 6.7 %copy-start.18 = (bf16[256]{0:T(256)(128)(2,1)S(1)}, bf16[256]{0:T(256)(128)(2,1)}, u32[]{:S(2)}) copy-start(bf16[256]{0:T(256)(128)(2,1)} %param.29) | copy-start | bytes 1540
  7.2 6.7 %copy-start.19 = (bf16[256]{0:T(256)(128)(2,1)S(1)}, bf16[256]{0:T(256)(128)(2,1)}, u32[]{:S(2)}) copy-start(bf16[256]{0:T(256)(128)(2,1)} %param.28) | copy-start | bytes 1540
  7.2 6.7 %copy-start.17 = (bf16[256]{0:T(256)(128)(2,1)S(1)}, bf16[256]{0:T(256)(128)(2,1)}, u32[]{:S(2)}) copy-start(bf16[256]{0:T(256)(128)(2,1)} %param.27) | copy-start | bytes 1540
  7.2 6.7 %copy-start.16 = (bf16[256]{0:T(256)(128)(2,1)S(1)}, bf16[256]{0:T(256)(128)(2,1)}, u32[]{:S(2)}) copy-start(bf16[256]{0:T(256)(128)(2,1)} %param.25) | copy-start | bytes 1540
  7.2 6.7 %copy-start.15 = (bf16[256]{0:T(256)(128)(2,1)S(1)}, bf16[256]{0:T(256)(128)(2,1)}, u32[]{:S(2)}) copy-start(bf16[256]{0:T(256)(128)(2,1)} %param.24) | copy-start | bytes 1540
  7.2 6.7 %copy-start.14 = (bf16[256]{0:T(256)(128)(2,1)S(1)}, bf16[256]{0:T(256)(128)(2,1)}, u32[]{:S(2)}) copy-start(bf16[256]{0:T(256)(128)(2,1)} %param.23) | copy-start | bytes 1540
  7.3 6.7 %copy-start.13 = (bf16[256]{0:T(256)(128)(2,1)S(1)}, bf16[256]{0:T(256)(128)(2,1)}, u32[]{:S(2)}) copy-start(bf16[256]{0:T(256)(128)(2,1)} %param.22) | copy-start | bytes 1540
  7.3 77.6 %all-gather.4.cloned.1.call-start = ((), (), s32[]{:S(2)}) async-start(), calls=%async_computation.4 | async-start | bytes 2359296 | tf_op jit(solution)/shard_map/all_gather | solution.py:928
  8.0 195.8 %all-gather.6.cloned.1.call-start = ((), (), s32[]{:S(2)}) async-start(), calls=%async_computation.5 | async-start | bytes 9437184 | tf_op jit(solution)/shard_map/all_gather | solution.py:929
  8.7 195.0 %all-gather.8.cloned.1.call-start = ((), (), s32[]{:S(2)}) async-start(), calls=%async_computation.6 | async-start | bytes 9437184 | tf_op jit(solution)/shard_map/all_gather | solution.py:930
  9.5 606.6 %reduce-scatter.7.cloned.1.call-start = ((), (), s32[]{:S(2)}) async-start(), calls=%async_computation.8 | async-start | bytes 2359296 | tf_op jit(solution)/shard_map/reduce_scatter | solution.py:1056
  14.0 2.2 copy-start.2
  62.0 1.7 copy-start
  63.7 2.0 copy-start.6
  66.9 11.3 %copy-start.7 = (f32[1,1,8,256]{3,1,2,0:T(1,128)}, f32[1,1,8,256]{3,1,2,0:T(1,128)S(1)}, u32[]{:S(2)}) copy-start(f32[1,1,8,256]{3,1,2,0:T(1,128)S(1)} %copy.47) | copy-start | bytes 24580
  78.8 6.0 copy-start.5
  84.9 1.6 copy-start.3
  201.8 2.0 copy-start.1
  345.0 6.4 %copy-start.4 = (bf16[512,2048]{1,0:T(8,128)(2,1)S(1)}, bf16[512,2048]{1,0:T(8,128)(2,1)}, u32[]{:S(2)}) copy-start(bf16[512,2048]{1,0:T(8,128)(2,1)} %all-gather.4.cloned.1.call-done.w_ref) | copy-start | bytes 6291460
  351.4 266.5 %reduce-scatter.5.cloned.1.call-start = ((), (), s32[]{:S(2)}) async-start(), calls=%async_computation.7 | async-start | bytes 7077888 | tf_op jit(solution)/shard_map/reduce_scatter | solution.py:1056
  381.9 239.1 %reduce-scatter.11.cloned.1.call-start = ((), (), s32[]{:S(2)}) async-start(), calls=%async_computation.10 | async-start | bytes 9437184 | tf_op jit(solution)/shard_map/reduce_scatter | solution.py:1056
  382.4 241.2 %reduce-scatter.9.cloned.1.call-start = ((), (), s32[]{:S(2)}) async-start(), calls=%async_computation.9 | async-start | bytes 9437184 | tf_op jit(solution)/shard_map/reduce_scatter | solution.py:1056
  382.5 0.7 copy-start.9
  382.5 1.3 copy-start.11
  382.5 1.3 copy-start.10
  382.5 1.3 copy-start.8
  382.5 2.0 copy-start.12
Sparse Core Ops, SparseCore 0:
  9.9 39.9 all-gather.3
  51.9 54.4 all-gather.5
  108.2 55.8 all-gather.7
  351.5 39.3 reduce-scatter.6
  394.2 61.8 reduce-scatter.4
  459.4 71.2 reduce-scatter.10
  534.2 71.4 reduce-scatter.8
